TPU v7x, 32 devices: a 4x4x1 block of a 4x4x8 slice. The times are simulated.
32 devices in a mesh: rep: 1 (over z), data: 4 (over y), model: 8 (over x, core).
Axes of the slice: x: 4, y: 4, z: 1, core: 2. Of those that a mesh axis runs over, the one named last changes fastest.
The devices are a block of a 4x4x8 slice.
Arguments:
- x_in: bfloat16 [8, 1024, 4096], P(('rep', 'data'), 'model')
- key_lens: int32 [8], P(('rep', 'data'))
- ln_gain: bfloat16 [2, 4096], P(None, 'data')
- w_in: bfloat16 [2, 4096, 40960], P(None, 'data', 'model')
- w_out_attn: bfloat16 [2, 4096, 4096], P(None, 'model', 'data')
- w_out_mlp: bfloat16 [2, 16384, 4096], P(None, 'model', 'data')
Outputs:
- output: bfloat16 [8, 1024, 4096], P(('rep', 'data'), 'model')
All inputs are finite; a program needn't handle non-finite values.
Results may differ from a plain program's by a relative error of at most 0.0171323.
Values are sent between devices in bfloat16 or wider.
A program may use at most 768 MiB of HBM per device.

v0:
```python
import jax
import jax.numpy as jnp
from jax import lax
from jax.sharding import PartitionSpec as P, NamedSharding

EPSILON = 1e-6


def layer_norm(act_in, gain_vec):
    act_f32 = act_in.astype(jnp.float32)
    row_mean = jnp.mean(act_f32, axis=-1, keepdims=True)
    centered = act_f32 - row_mean
    row_var = jnp.mean(centered * centered, axis=-1, keepdims=True)
    return (centered * lax.rsqrt(row_var + EPSILON) * gain_vec.astype(jnp.float32)).astype(jnp.bfloat16)


def solution(mesh):
    n_groups = mesh.shape['model']
    batch_axes = ('rep', 'data')

    def device_step(x_loc, len_loc, gain_loc, w_in_loc, w_attn_loc, w_mlp_loc):
        n_layers = w_in_loc.shape[0]
        block_in = w_in_loc.shape[2]
        attn_width = w_attn_loc.shape[1]
        ff_local = w_mlp_loc.shape[1]
        head_dim = (block_in - attn_width - 2 * ff_local) // 2
        q_group = attn_width // head_dim
        batch_loc, seq_loc = x_loc.shape[0], x_loc.shape[1]
        seq_len = seq_loc * n_groups
        kv_start = attn_width
        ff_start = attn_width + 2 * head_dim
        positions = jnp.arange(seq_len)
        allowed = (positions[None, :] <= positions[:, None])[None, :, :] & (positions[None, None, :] < len_loc[:, None, None])
        allowed = allowed[:, None, :, :]
        hidden = x_loc
        for layer_idx in range(n_layers):
            gain_full = lax.all_gather(gain_loc[layer_idx], 'data', axis=0, tiled=True)
            w_in_full = lax.all_gather(w_in_loc[layer_idx], 'data', axis=0, tiled=True)
            w_attn_full = lax.all_gather(w_attn_loc[layer_idx], 'data', axis=1, tiled=True)
            w_mlp_full = lax.all_gather(w_mlp_loc[layer_idx], 'data', axis=1, tiled=True)
            normed = layer_norm(hidden, gain_full)
            h_full = lax.all_gather(normed, 'model', axis=1, tiled=True)
            projected = jnp.dot(h_full, w_in_full, preferred_element_type=jnp.float32).astype(jnp.bfloat16)
            queries = projected[:, :, :attn_width].reshape(batch_loc, seq_len, q_group, head_dim)
            key_head = projected[:, :, kv_start:kv_start + head_dim]
            value_head = projected[:, :, kv_start + head_dim:ff_start]
            gate_proj = projected[:, :, ff_start:ff_start + ff_local]
            up_proj = projected[:, :, ff_start + ff_local:]
            scores = jnp.einsum('crke,cle->ckrl', queries, key_head, preferred_element_type=jnp.float32) * head_dim ** -0.5
            scores = jnp.where(allowed, scores, -1e30)
            soft_probs = jax.nn.softmax(scores, axis=-1)
            attn_heads = jnp.einsum('ckrl,cle->crke', soft_probs, value_head, preferred_element_type=jnp.float32).astype(jnp.bfloat16)
            attn_heads = attn_heads.reshape(batch_loc, seq_len, attn_width)
            mlp_act = (jax.nn.silu(gate_proj.astype(jnp.float32)) * up_proj.astype(jnp.float32)).astype(jnp.bfloat16)
            group_part = (jnp.dot(attn_heads, w_attn_full, preferred_element_type=jnp.float32) + jnp.dot(mlp_act, w_mlp_full, preferred_element_type=jnp.float32)).astype(jnp.bfloat16)
            z_loc = lax.psum_scatter(group_part, 'model', scatter_dimension=1, tiled=True)
            hidden = (hidden.astype(jnp.float32) + z_loc.astype(jnp.float32)).astype(jnp.bfloat16)
        return hidden

    return jax.shard_map(device_step, mesh=mesh, in_specs=(P(batch_axes, 'model', None), P(batch_axes), P(None, 'data'), P(None, 'data', 'model'), P(None, 'model', 'data'), P(None, 'model', 'data')), out_specs=P(batch_axes, 'model', None), check_vma=False)
```

profile of v0, /device:TPU:97, one launch (start us, length us, event | category | flops | bytes accessed | tf_op | source)
XLA Modules:
  0.0 1622.7 jit_solution(14363728487029163807)
XLA Ops:
  7.9 11.6 all-gather
  27.7 16.3 %fusion.83 = (bf16[1,1024,5120]{2,1,0:T(8,128)(2,1)}, bf16[1,1024,5120]{2,1,0:T(8,128)(2,1)}) fusion(bf16[2,1024,5120]{2,1,0:T(8,128)(2,1)} %param.9), kind=kLoop, calls=%fused_computation.99 | loop fusion | bytes 41943040 | tf_op jit(solution)/shard_map/slice | solution.py:38
  44.2 6.1 fusion.84
  55.0 59.9 %all-gather.17.cloned.1.call-done = bf16[2,1024,4096]{2,1,0:T(8,128)(2,1)} async-done(((bf16[2,128,4096]{2,1,0:T(8,128)(2,1)}), bf16[2,1024,4096]{2,1,0:T(8,128)(2,1)}) %all-gather.17.cloned.1.call-update) | async-done | bytes 16777232 | tf_op jit(solution)/shard_map/all_gather | solution.py:42
  115.0 363.0 %all-gather.21.cloned.1.call-done = bf16[1,4096,5120]{2,1,0:T(8,128)(2,1)} async-done(((bf16[1,1024,5120]{2,1,0:T(8,128)(2,1)}), bf16[1,4096,5120]{2,1,0:T(8,128)(2,1)}) %all-gather.21.cloned.1.call-update) | async-done | bytes 41943056 | tf_op jit(solution)/shard_map/all_gather | solution.py:38
  478.0 95.8 %fusion.24 = bf16[2,1024,5120]{2,1,0:T(8,128)(2,1)} fusion(bf16[2,1024,4096]{2,1,0:T(8,128)(2,1)} %all-gather.17.cloned.1.call-done, bf16[1,4096,5120]{2,1,0:T(8,128)(2,1)} %all-gather.21.cloned.1.call-done), kind=kOutput, calls=%fused_computation.34 | convolution fusion | flops 85909831680 | bytes 79691776 | tf_op jit(solution)/shard_map/dot_general | solution.py:43
  573.8 58.9 %all-gather.25.cloned.1.call-done = bf16[1,2048,4096]{2,1,0:T(8,128)(2,1)} async-done(((bf16[1,2048,1024]{2,1,0:T(8,128)(2,1)}), bf16[1,2048,4096]{2,1,0:T(8,128)(2,1)}) %all-gather.25.cloned.1.call-update) | async-done | bytes 16777232 | tf_op jit(solution)/shard_map/all_gather | solution.py:40
  632.7 47.2 %fusion.14 = f32[2,1024,4096]{2,1,0:T(8,128)} fusion(bf16[1,2048,4096]{2,1,0:T(8,128)(2,1)} %all-gather.25.cloned.1.call-done, bf16[2,1024,5120]{2,1,0:T(8,128)(2,1)} %fusion.24), kind=kOutput, calls=%fused_computation.21 | convolution fusion | flops 34393292800 | bytes 67108864 | tf_op jit(solution)/shard_map/dot_general | solution.py:55
  679.9 8.9 fusion.30
  688.8 8.1 fusion.22
  699.4 8.0 fusion.70
  707.4 23.6 %add_convert_fusion.1 = bf16[2,1024,4096]{2,1,0:T(8,128)(2,1)} fusion(f32[2,1024,4096]{2,1,0:T(8,128)} %fusion.14, bf16[2,1024,512]{1,2,0:T(8,128)(2,1)} %bitcast.103, bf16[1,512,4096]{2,1,0:T(8,128)(2,1)} %all-gather.23.cloned.1.call-done), kind=kOutput, calls=%fused_computation.5 | convolution fusion | flops 8606711808 | bytes 56623104 | tf_op jit(solution)/shard_map/dot_general | solution.py:55
  731.8 9.0 all-gather.4
  740.8 80.4 %reduce-scatter.3.cloned.1.call-done = bf16[2,128,4096]{2,1,0:T(8,128)(2,1)} async-done(((bf16[2,1024,4096]{2,1,0:T(8,128)(2,1)}), bf16[2,128,4096]{2,1,0:T(8,128)(2,1)}) %reduce-scatter.3.cloned.1.call-update) | async-done | bytes 2097168 | tf_op jit(solution)/shard_map/reduce_scatter | solution.py:56
  828.8 355.2 %all-gather.27.cloned.1.call-done = bf16[1,4096,5120]{2,1,0:T(8,128)(2,1)} async-done(((bf16[1,1024,5120]{2,1,0:T(8,128)(2,1)}), bf16[1,4096,5120]{2,1,0:T(8,128)(2,1)}) %all-gather.27.cloned.1.call-update) | async-done | bytes 41943056 | tf_op jit(solution)/shard_map/all_gather | solution.py:38
  1184.1 85.6 %all-gather.19.cloned.1.call-done = bf16[2,1024,4096]{2,1,0:T(8,128)(2,1)} async-done(((bf16[2,128,4096]{2,1,0:T(8,128)(2,1)}), bf16[2,1024,4096]{2,1,0:T(8,128)(2,1)}) %all-gather.19.cloned.1.call-update) | async-done | bytes 16777232 | tf_op jit(solution)/shard_map/all_gather | solution.py:42
  1269.7 95.9 %fusion.27 = bf16[2,1024,5120]{2,1,0:T(8,128)(2,1)} fusion(bf16[2,1024,4096]{2,1,0:T(8,128)(2,1)} %all-gather.19.cloned.1.call-done, bf16[1,4096,5120]{2,1,0:T(8,128)(2,1)} %all-gather.27.cloned.1.call-done), kind=kOutput, calls=%fused_computation.35 | convolution fusion | flops 85909831680 | bytes 79691776 | tf_op jit(solution)/shard_map/dot_general | solution.py:43
  1365.6 58.0 %all-gather.31.cloned.1.call-done = bf16[1,2048,4096]{2,1,0:T(8,128)(2,1)} async-done(((bf16[1,2048,1024]{2,1,0:T(8,128)(2,1)}), bf16[1,2048,4096]{2,1,0:T(8,128)(2,1)}) %all-gather.31.cloned.1.call-update) | async-done | bytes 16777232 | tf_op jit(solution)/shard_map/all_gather | solution.py:40
  1423.6 47.2 %fusion.12 = f32[2,1024,4096]{2,1,0:T(8,128)} fusion(bf16[1,2048,4096]{2,1,0:T(8,128)(2,1)} %all-gather.31.cloned.1.call-done, bf16[2,1024,5120]{2,1,0:T(8,128)(2,1)} %fusion.27), kind=kOutput, calls=%fused_computation.18 | convolution fusion | flops 34393292800 | bytes 67108864 | tf_op jit(solution)/shard_map/dot_general | solution.py:55
  1470.8 8.9 fusion.31
  1479.7 8.1 fusion.23
  1490.3 8.0 fusion.73
  1498.2 23.4 %add_convert_fusion = bf16[2,1024,4096]{2,1,0:T(8,128)(2,1)} fusion(f32[2,1024,4096]{2,1,0:T(8,128)} %fusion.12, bf16[2,1024,512]{1,2,0:T(8,128)(2,1)} %bitcast.102, bf16[1,512,4096]{2,1,0:T(8,128)(2,1)} %all-gather.29.cloned.1.call-done), kind=kOutput, calls=%fused_computation.4 | convolution fusion | flops 8606711808 | bytes 56623104 | tf_op jit(solution)/shard_map/dot_general | solution.py:55
  1521.7 90.2 %reduce-scatter.5.cloned.1.call-done = bf16[2,128,4096]{2,1,0:T(8,128)(2,1)} async-done(((bf16[2,1024,4096]{2,1,0:T(8,128)(2,1)}), bf16[2,128,4096]{2,1,0:T(8,128)(2,1)}) %reduce-scatter.5.cloned.1.call-update) | async-done | bytes 2097168 | tf_op jit(solution)/shard_map/reduce_scatter | solution.py:56
  (64 shorter events, 31.5 us)
Async XLA Ops:
  6.5 108.4 %all-gather.17.cloned.1.call-start = ((), (), s32[]{:S(2)}) async-start(), calls=%async_computation.2 | async-start | bytes 18874368 | tf_op jit(solution)/shard_map/all_gather | solution.py:42
  27.6 450.4 %all-gather.21.cloned.1.call-start = ((), (), s32[]{:S(2)}) async-start(), calls=%async_computation.6 | async-start | bytes 52428800 | tf_op jit(solution)/shard_map/all_gather | solution.py:38
  44.0 6.3 copy-start.7
  44.0 8.8 copy-start.9
  44.1 588.6 %all-gather.25.cloned.1.call-start = ((), (), s32[]{:S(2)}) async-start(), calls=%async_computation.8 | async-start | bytes 20971520 | tf_op jit(solution)/shard_map/all_gather | solution.py:40
  50.3 657.1 %all-gather.23.cloned.1.call-start = ((), (), s32[]{:S(2)}) async-start(), calls=%async_computation.7 | async-start | bytes 5242880 | tf_op jit(solution)/shard_map/all_gather | solution.py:39
  51.9 769.3 %reduce-scatter.3.cloned.1.call-start = ((), (), s32[]{:S(2)}) async-start(), calls=%async_computation.3 | async-start | bytes 18874368 | tf_op jit(solution)/shard_map/reduce_scatter | solution.py:56
  573.8 106.1 %copy-start.3 = (pred[2,1024,1024]{1,2,0:T(8,128)(4,1)S(1)}, pred[2,1024,1024]{1,2,0:T(8,128)(4,1)}, u32[]{:S(2)}) copy-start(pred[2,1024,1024]{1,2,0:T(8,128)(4,1)} %broadcast_and_fusion) | copy-start | bytes 6291460
  632.7 47.2 %slice-start = ((bf16[2,1024,5120]{2,1,0:T(8,128)(2,1)}), bf16[2,1024,512]{2,1,0:T(8,128)(2,1)S(1)}, s32[]{:S(2)}) async-start(bf16[2,1024,5120]{2,1,0:T(8,128)(2,1)} %fusion.24), calls=%async_computation.12 | async-start | bytes 4194304 | tf_op jit(solution)/shard_map/slice | solution.py:44
  688.8 10.6 copy-start.6
  731.0 0.8 copy-start.8
  731.0 90.2 %copy-start.2 = (bf16[2,128,4096]{2,1,0:T(8,128)(2,1)S(1)}, bf16[2,128,4096]{2,1,0:T(8,128)(2,1)}, u32[]{:S(2)}) copy-start(bf16[2,128,4096]{2,1,0:T(8,128)(2,1)} %param.6) | copy-start | bytes 6291460
  731.1 453.0 %all-gather.27.cloned.1.call-start = ((), (), s32[]{:S(2)}) async-start(), calls=%async_computation.9 | async-start | bytes 52428800 | tf_op jit(solution)/shard_map/all_gather | solution.py:38
  731.7 538.0 %all-gather.19.cloned.1.call-start = ((), (), s32[]{:S(2)}) async-start(), calls=%async_computation.4 | async-start | bytes 18874368 | tf_op jit(solution)/shard_map/all_gather | solution.py:42
  823.6 1.3 copy-start
  827.2 596.4 %all-gather.31.cloned.1.call-start = ((), (), s32[]{:S(2)}) async-start(), calls=%async_computation.11 | async-start | bytes 20971520 | tf_op jit(solution)/shard_map/all_gather | solution.py:40
  828.0 670.2 %all-gather.29.cloned.1.call-start = ((), (), s32[]{:S(2)}) async-start(), calls=%async_computation.10 | async-start | bytes 5242880 | tf_op jit(solution)/shard_map/all_gather | solution.py:39
  828.8 783.1 %reduce-scatter.5.cloned.1.call-start = ((), (), s32[]{:S(2)}) async-start(), calls=%async_computation.5 | async-start | bytes 18874368 | tf_op jit(solution)/shard_map/reduce_scatter | solution.py:56
  1365.6 105.2 %copy-start.4 = (pred[2,1024,1024]{1,2,0:T(8,128)(4,1)S(1)}, pred[2,1024,1024]{1,2,0:T(8,128)(4,1)}, u32[]{:S(2)}) copy-start(pred[2,1024,1024]{1,2,0:T(8,128)(4,1)} %broadcast_and_fusion) | copy-start | bytes 6291460
  1423.6 47.2 %slice-start.1 = ((bf16[2,1024,5120]{2,1,0:T(8,128)(2,1)}), bf16[2,1024,512]{2,1,0:T(8,128)(2,1)S(1)}, s32[]{:S(2)}) async-start(bf16[2,1024,5120]{2,1,0:T(8,128)(2,1)} %fusion.27), calls=%async_computation.13 | async-start | bytes 4194304 | tf_op jit(solution)/shard_map/slice | solution.py:44
  1479.7 10.6 copy-start.5
  1521.7 90.2 %copy-start.1 = (bf16[2,128,4096]{2,1,0:T(8,128)(2,1)S(1)}, bf16[2,128,4096]{2,1,0:T(8,128)(2,1)}, u32[]{:S(2)}) copy-start(bf16[2,128,4096]{2,1,0:T(8,128)(2,1)} %copy-done) | copy-start | bytes 6291460
Sparse Core Ops, SparseCore 0:
  27.7 87.1 all-gather.16
  116.5 361.4 all-gather.20
  479.6 153.0 all-gather.24
  634.1 46.4 all-gather.22
  731.2 89.9 reduce-scatter.2
  822.6 361.3 all-gather.26
  1185.7 83.9 all-gather.18
  1271.3 152.2 all-gather.30
  1425.1 46.4 all-gather.28
  1521.9 90.0 reduce-scatter.4
where the time goes:
time: 1630 us; the launch traced here: 1620 us
  waiting for transfers between devices  1150 us (71%)
  matrix products  367 us (23%)
  other arithmetic  35.7 us (2%)
  local copies, waits for them, and re-layouts  30.9 us (2%)
  blocking collectives  20.6 us (1%)
    all_gather x2, waiting for transfers between devices, device_step(): w_in_full = lax.all_gather(w_in_loc[layer_idx], 'data', axis=0, tiled=True)  718 us
    dot_general x2, matrix products, device_step(): jnp.dot(h_full, w_in_full, preferred_element_type=jnp.float32)  192 us
    reduce_scatter x2, waiting for transfers between devices, device_step(): lax.psum_scatter(group_part, 'model', scatter_dimension=1, tiled=True)  171 us
    all_gather x2, waiting for transfers between devices, device_step(): h_full = lax.all_gather(normed, 'model', axis=1, tiled=True)  146 us
    all_gather x2, waiting for transfers between devices, device_step(): lax.all_gather(w_mlp_loc[layer_idx], 'data', axis=1, tiled=True)  117 us
    dot_general x2, matrix products, device_step(): jnp.dot(mlp_act, w_mlp_full, preferred_element_type=jnp.float32)  94.5 us
    dot_general x2, matrix products, device_step(): jnp.dot(attn_heads, w_attn_full, preferred_element_type=jnp.float32)  47.1 us
  transfers between devices with their start and end apart: 10, of which 8 were waited for; matrix products, arithmetic and copies ran while one was open for 23% of the time, Pallas kernels for 0%

commit v1 on v0

v1 whole, which is shorter than its diff:
```python
import jax
import jax.numpy as jnp
from jax import lax
from jax.experimental import pallas as pl
from jax.experimental.pallas import tpu as pltpu
from jax.sharding import PartitionSpec as P


EPSILON = 1e-6
BOTH = ('data', 'model')


def layer_norm(act_in, gain_vec):
    act_f32 = act_in.astype(jnp.float32)
    row_mean = jnp.mean(act_f32, axis=-1, keepdims=True)
    centered = act_f32 - row_mean
    row_var = jnp.mean(centered * centered, axis=-1, keepdims=True)
    return (centered * lax.rsqrt(row_var + EPSILON) * gain_vec.astype(jnp.float32)).astype(jnp.bfloat16)


def matmul(lhs, rhs):
    return jnp.dot(lhs, rhs, preferred_element_type=jnp.float32)


def project(h_seq, slab_ids, ours, theirs, total_in, final):
    n_slabs = len(ours)
    rows, cols = h_seq.shape[0], ours[0].shape[1]
    depth = ours[0].shape[0]
    tile, chunk = 512, 512
    tiles = cols // tile
    out_dtype = jnp.bfloat16 if final else jnp.float32

    def kernel(ids_ref, *refs):
        h_refs, w_refs, rest = refs[:n_slabs], refs[n_slabs:3 * n_slabs], refs[3 * n_slabs:]

        def run(w_half):
            @pl.loop(0, rows // chunk)
            def _(step):
                at = pl.ds(pl.multiple_of(step * chunk, chunk), chunk)
                total = matmul(h_refs[0][at, :], w_half[0][...])
                for h_ref, w_ref in zip(h_refs[1:], w_half[1:]):
                    total = total + matmul(h_ref[at, :], w_ref[...])
                if len(rest) == 2:
                    total = total + rest[0][0, at, :]
                rest[-1][0, at, :] = total.astype(out_dtype)

        @pl.when(pl.program_id(0) == 0)
        def _():
            run(w_refs[:n_slabs])

        @pl.when(pl.program_id(0) == 1)
        def _():
            run(w_refs[n_slabs:])

    in_specs = [pl.BlockSpec((rows, depth), lambda p, n, ids, i=i: (0, ids[i])) for i in range(n_slabs)]
    in_specs += [pl.BlockSpec((depth, tile), lambda p, n, ids: (0, jnp.where(p == 0, n, tiles - 1)))] * n_slabs
    in_specs += [pl.BlockSpec((depth, tile), lambda p, n, ids: (0, jnp.where(p == 0, 0, n)))] * n_slabs
    wide = pl.BlockSpec((1, rows, tile), lambda p, n, ids: (p, 0, n))
    args = [h_seq] * n_slabs + list(ours) + list(theirs)
    if total_in is not None:
        in_specs.append(wide)
        args.append(total_in)
    out_shape = jax.ShapeDtypeStruct((2, rows, cols), out_dtype)
    flops = 2 * 2 * n_slabs * rows * depth * cols
    return pl.pallas_call(
        kernel,
        out_shape=out_shape,
        grid_spec=pltpu.PrefetchScalarGridSpec(num_scalar_prefetch=1, grid=(2, tiles), in_specs=in_specs, out_specs=wide),
        cost_estimate=pl.CostEstimate(flops=flops, bytes_accessed=2 * n_slabs * depth * (rows + 2 * cols) + 4 * rows * cols, transcendentals=0),
    )(jnp.stack(slab_ids).astype(jnp.int32), *args)


def mix_out(attn, mlp, w_ours, w_theirs):
    n_seq = len(attn)
    _, rows, q_cut = attn[0].shape
    ff = mlp[0].shape[2]
    cols = w_ours.shape[1]
    chunk = 512
    steps = rows // chunk

    def kernel(*refs):
        lhs, (wa_ref, wb_ref, out_ref) = refs[:-3], refs[-3:]

        def run(a_ref, m_ref):
            total = matmul(a_ref[0], wa_ref[:q_cut, :]) + matmul(m_ref[0], wa_ref[q_cut:, :])
            total = total + matmul(a_ref[1], wb_ref[:q_cut, :]) + matmul(m_ref[1], wb_ref[q_cut:, :])
            out_ref[0] = total.astype(jnp.bfloat16)

        for b in range(n_seq):
            @pl.when(pl.program_id(0) == b)
            def _(b=b):
                run(lhs[2 * b], lhs[2 * b + 1])

    in_specs, args = [], []
    for b in range(n_seq):
        for arr in (attn[b], mlp[b]):
            in_specs.append(pl.BlockSpec((2, chunk, arr.shape[2]), lambda s, m, b=b: (0, jnp.where(s == b, m, jnp.where(s < b, 0, steps - 1)), 0)))
            args.append(arr)
    in_specs += [pl.BlockSpec(w_ours.shape, lambda s, m: (0, 0))] * 2
    return pl.pallas_call(
        kernel,
        out_shape=jax.ShapeDtypeStruct((n_seq, rows, cols), jnp.bfloat16),
        grid=(n_seq, steps),
        in_specs=in_specs,
        out_specs=pl.BlockSpec((1, chunk, cols), lambda s, m: (s, m, 0)),
        cost_estimate=pl.CostEstimate(flops=4 * n_seq * rows * (q_cut + ff) * cols, bytes_accessed=4 * n_seq * rows * (q_cut + ff) + 4 * w_ours.size + 2 * n_seq * rows * cols, transcendentals=0),
    )(*args, w_ours, w_theirs)


def attend(both, core, key_len, head_dim):
    _, rows, _ = both.shape
    chunk = 256

    def kernel(nums_ref, q_ref, k_ref, v_ref, out_ref):
        start = pl.program_id(1) * chunk
        scores = lax.dot_general(q_ref[0], k_ref[0], (((1,), (1,)), ((), ())), preferred_element_type=jnp.float32) * head_dim ** -0.5
        q_pos = start + lax.broadcasted_iota(jnp.int32, scores.shape, 0)
        k_pos = lax.broadcasted_iota(jnp.int32, scores.shape, 1)
        scores = jnp.where((k_pos <= q_pos) & (k_pos < nums_ref[1]), scores, -1e30)
        weights = jnp.exp(scores - jnp.max(scores, axis=-1, keepdims=True))
        norm = jnp.sum(weights, axis=-1, keepdims=True)
        probs = weights / norm
        out = jnp.dot(probs, v_ref[0].astype(jnp.float32), preferred_element_type=jnp.float32)
        out_ref[0] = out.astype(jnp.bfloat16)

    return pl.pallas_call(
        kernel,
        out_shape=jax.ShapeDtypeStruct((2, rows, head_dim), jnp.bfloat16),
        grid_spec=pltpu.PrefetchScalarGridSpec(
            num_scalar_prefetch=1,
            grid=(2, rows // chunk),
            in_specs=[
                pl.BlockSpec((1, chunk, head_dim), lambda j, m, nums: (j, m, 0)),
                pl.BlockSpec((1, rows, head_dim), lambda j, m, nums: (nums[0], 0, 1)),
                pl.BlockSpec((1, rows, head_dim), lambda j, m, nums: (1 - nums[0], 0, 1)),
            ],
            out_specs=pl.BlockSpec((1, chunk, head_dim), lambda j, m, nums: (j, m, 0)),
        ),
        cost_estimate=pl.CostEstimate(flops=8 * rows * rows * head_dim, bytes_accessed=16 * rows * head_dim, transcendentals=2 * rows * rows),
    )(jnp.stack([core, key_len]).astype(jnp.int32), both, both, both)


def split_columns(w_in, layer_idx, core, head_dim, q_group, ff_half):
    _, rows, width = w_in.shape
    tile = head_dim
    ff_tiles = ff_half // tile
    n_tiles = width // tile // 2

    def source(n, j):
        gate = q_group + 2 + j * ff_tiles + (n - 2)
        up = q_group + 2 + 2 * ff_tiles + j * ff_tiles + (n - 2 - ff_tiles)
        return jnp.where(n == 0, j, jnp.where(n == 1, q_group + j, jnp.where(n < 2 + ff_tiles, gate, up)))

    def kernel(core_ref, own_ref, other_ref, own_out, other_out):
        own_out[...] = own_ref[0]
        other_out[...] = other_ref[0]

    out = pl.BlockSpec((rows, tile), lambda n, c: (0, n))
    return pl.pallas_call(
        kernel,
        out_shape=[jax.ShapeDtypeStruct((rows, width // 2), w_in.dtype)] * 2,
        grid_spec=pltpu.PrefetchScalarGridSpec(
            num_scalar_prefetch=1,
            grid=(n_tiles,),
            in_specs=[
                pl.BlockSpec((1, rows, tile), lambda n, c: (layer_idx, 0, source(n, c[0]))),
                pl.BlockSpec((1, rows, tile), lambda n, c: (layer_idx, 0, source(n, 1 - c[0]))),
            ],
            out_specs=[out, out],
        ),
        cost_estimate=pl.CostEstimate(flops=rows * width * 8, bytes_accessed=4 * rows * width, transcendentals=0),
    )(core.reshape(1).astype(jnp.int32), w_in, w_in)


def split_rows(w_attn, w_mlp, layer_idx, core):
    _, q_rows, cols = w_attn.shape
    ff = w_mlp.shape[1]
    q_half, ff_half = q_rows // 2, ff // 2
    tile = q_half
    n_tiles = 1 + ff_half // tile

    def kernel(core_ref, own_a, own_m, other_a, other_m, own_out, other_out):
        @pl.when(pl.program_id(0) == 0)
        def _():
            own_out[...] = own_a[0]
            other_out[...] = other_a[0]

        @pl.when(pl.program_id(0) > 0)
        def _():
            own_out[...] = own_m[0]
            other_out[...] = other_m[0]

    def a_spec(flip):
        return pl.BlockSpec((1, tile, cols), lambda n, c: (layer_idx, 1 - c[0] if flip else c[0], 0))

    def m_spec(flip):
        return pl.BlockSpec((1, tile, cols), lambda n, c: (layer_idx, (1 - c[0] if flip else c[0]) * (ff_half // tile) + jnp.maximum(n - 1, 0), 0))

    out = pl.BlockSpec((tile, cols), lambda n, c: (n, 0))
    return pl.pallas_call(
        kernel,
        out_shape=[jax.ShapeDtypeStruct((q_half + ff_half, cols), w_attn.dtype)] * 2,
        grid_spec=pltpu.PrefetchScalarGridSpec(
            num_scalar_prefetch=1,
            grid=(n_tiles,),
            in_specs=[a_spec(False), m_spec(False), a_spec(True), m_spec(True)],
            out_specs=[out, out],
        ),
        cost_estimate=pl.CostEstimate(flops=(q_rows + ff) * cols * 8, bytes_accessed=4 * (q_rows + ff) * cols, transcendentals=0),
    )(core.reshape(1).astype(jnp.int32), w_attn, w_mlp, w_attn, w_mlp)


def solution(mesh):
    n_data, n_model = mesh.shape['data'], mesh.shape['model']
    batch_axes = ('rep', 'data')
    last = n_data - 1

    def table(move):
        pairs = []
        for row in range(n_data):
            for col in range(n_model):
                to = move(row, col)
                if to is not None:
                    pairs.append((row * n_model + col, to[0] * n_model + to[1]))
        return pairs

    core_swap = table(lambda r, m: (r, m ^ 1))
    near_swap = table(lambda r, m: (r ^ 1, m))
    far_swap = table(lambda r, m: (last - r, m))
    spread_a = table(lambda r, m: (r ^ 1, m ^ 1) if m % 2 == 0 else (r, m ^ 1))
    spread_b = table(lambda r, m: None if m % 2 == 0 else (r ^ 1, m))
    collect_a = table(lambda r, m: (r, m ^ 1) if m % 2 == 0 else (r ^ 1, m ^ 1))
    lanes = [list(range(0, n_model, 2)), list(range(1, n_model, 2))]

    def send(val, pairs):
        return lax.ppermute(val, BOTH, pairs)

    def two_layers(x_loc, len_loc, gain_loc, w_in_loc, w_attn_loc, w_mlp_loc):
        n_layers, slab, block_in = w_in_loc.shape
        attn_width = w_attn_loc.shape[1]
        ff_local = w_mlp_loc.shape[1]
        head_dim = (block_in - attn_width - 2 * ff_local) // 2
        q_group = attn_width // head_dim
        batch_loc, seq_loc = x_loc.shape[0], x_loc.shape[1]
        ff_half = ff_local // 2
        row = lax.axis_index('data')
        core = lax.rem(lax.axis_index('model'), 2)
        even = core == 0
        wanted = lax.rem((row + 1) // 2, 2)
        mine_wanted = wanted == core
        slabs = (row, row ^ 1, last - row, (last - row) ^ 1)

        work_lens = jnp.where(even, len_loc, send(len_loc, near_swap))
        gain_all = lax.all_gather(gain_loc, 'data', axis=1, tiled=True)

        def pieces(keep_half, give_half):
            other = send(give_half, core_swap)
            keep = jnp.where(mine_wanted, keep_half, other)
            give = jnp.where(mine_wanted, other, keep_half)
            near = send(give, near_swap)
            far = send(keep, far_swap)
            far_near = send(near, far_swap)
            ours = (keep, near, far, far_near)
            theirs = tuple(send(p, core_swap) for p in ours)
            return ours, theirs

        hidden = x_loc
        w_pieces = []
        for layer_idx in range(n_layers):
            ins = pieces(*split_columns(w_in_loc, layer_idx, core, head_dim, q_group, ff_half))
            outs = pieces(*split_rows(w_attn_loc, w_mlp_loc, layer_idx, core))
            w_pieces.append((ins, outs))

        for layer_idx in range(n_layers):
            ins, outs = w_pieces[layer_idx]
            normed = layer_norm(hidden, gain_all[layer_idx])
            h_seqs = []
            for b in range(batch_loc):
                got_a = send(normed[b], spread_a)
                got_b = send(normed[b], spread_b)
                pair = jnp.concatenate([jnp.where(even, normed[b], got_a), jnp.where(even, got_a, got_b)], axis=0)
                h_seqs.append(lax.all_gather(pair, 'model', axis=0, tiled=True, axis_index_groups=lanes))
            firsts_in, totals = (ins[0][:3], ins[1][:3]), []
            for b in range(batch_loc):
                totals.append(project(h_seqs[b], slabs[:3], *firsts_in, None, False))
            attn_all, mlp_all = [], []
            for b in range(batch_loc):
                both = project(h_seqs[b], slabs[3:], ins[0][3:], ins[1][3:], totals[b], True)
                ff_at = attn_width // 2 + head_dim
                attn_all.append(attend(both, core, work_lens[b], head_dim))
                gate, up = both[:, :, ff_at:ff_at + ff_half], both[:, :, ff_at + ff_half:]
                mlp_all.append((jax.nn.silu(gate.astype(jnp.float32)) * up.astype(jnp.float32)).astype(jnp.bfloat16))
            firsts, seconds = [], []
            for i in range(n_data):
                part = mix_out(attn_all, mlp_all, outs[0][i], outs[1][i])
                pair = lax.psum_scatter(part, 'model', scatter_dimension=1, tiled=True, axis_index_groups=lanes)
                firsts.append(pair[:, :seq_loc])
                seconds.append(pair[:, seq_loc:])
            z_slabs = []
            for i in range(n_data):
                got_a = send(jnp.where(even, seconds[i], firsts[i ^ 1]), collect_a)
                got_b = send(seconds[i ^ 1], spread_b)
                z_slabs.append(jnp.where(even, firsts[i], got_b).astype(jnp.float32) + got_a.astype(jnp.float32))
            z_loc = jnp.zeros(hidden.shape, jnp.float32)
            for s, z in zip(slabs, z_slabs):
                z_loc = lax.dynamic_update_slice_in_dim(z_loc, z, s * slab, axis=2)
            hidden = (hidden.astype(jnp.float32) + z_loc).astype(jnp.bfloat16)
        return hidden

    return jax.shard_map(two_layers, mesh=mesh, in_specs=(P(batch_axes, 'model', None), P(batch_axes), P(None, 'data'), P(None, 'data', 'model'), P(None, 'model', 'data'), P(None, 'model', 'data')), out_specs=P(batch_axes, 'model', None), check_vma=False)
```

time: 1630 us -> 1570 us (0.963)
  Pallas kernels: 0 us -> 483 us
  matrix products: 367 us -> 0 us
  waiting for transfers between devices: 1150 us -> 884 us
  starting transfers between devices: 1.1 us -> 72.4 us
  other arithmetic: 35.7 us -> 79.8 us
    all_gather x8 -> x4, waiting for transfers between devices: 981 us -> 0.03 us  [two_layers(): lax.all_gather(pair, 'model', axis=0, tiled=True, axis_index_groups=lanes)]
    ppermute x0 -> x57, waiting for transfers between devices: none -> 812 us  [send(): return lax.ppermute(val, BOTH, pairs)]
    pallas_call x0 -> x24, Pallas kernels: none -> 483 us  [the longest x8 264 us: project(): pl.pallas_call(kernel, out_shape=out_shape, grid_spec=pltpu.PrefetchScala...]
    dot_general x10 -> x0, matrix products: 367 us -> none  [the longest x2 192 us: device_step(): jnp.dot(h_full, w_in_full, preferred_element_type=jnp.float32)]
    reduce_scatter x2 -> x8, waiting for transfers between devices: 171 us -> 71.2 us  [two_layers(): lax.psum_scatter(part, 'model', scatter_dimension=1, tiled=True, axis_ind...]
    ppermute x0 -> x57, starting transfers between devices: none -> 71.4 us  [send(): return lax.ppermute(val, BOTH, pairs)]
    select_n x0 -> x11, other arithmetic: none -> 35.6 us  [the longest x4 23.9 us: pieces(): keep = jnp.where(mine_wanted, keep_half, other)]
    slice x8 -> x1, local copies, waits for them, and re-layouts: 25.3 us -> 0.6 us  [two_layers(): attn_all.append(attend(both, core, work_lens[b], head_dim))]
  transfers between devices with their start and end apart: 10 -> 69, of which waited for: 8 -> 35; matrix products, arithmetic and copies ran while one was open for 23% -> 4% of each run, Pallas kernels for 0% -> 29%
where the time goes in v1:
time: 1570 us; the launch traced here: 1560 us
  waiting for transfers between devices  884 us (56%)
  Pallas kernels  483 us (31%)
  other arithmetic  79.8 us (5%)
  starting transfers between devices  72.4 us (5%)
  local copies, waits for them, and re-layouts  15.9 us (1%)
    ppermute x57, waiting for transfers between devices, send(): return lax.ppermute(val, BOTH, pairs)  812 us
    pallas_call x8, Pallas kernels, project(): pl.pallas_call(kernel, out_shape=out_shape, grid_spec=pltpu.PrefetchScala...  264 us
    pallas_call x8, Pallas kernels, mix_out(): pl.pallas_call(kernel, out_shape=jax.ShapeDtypeStruct((n_seq, rows, cols)...  137 us
    ppermute x57, starting transfers between devices, send(): return lax.ppermute(val, BOTH, pairs)  71.4 us
    reduce_scatter x8, waiting for transfers between devices, two_layers(): lax.psum_scatter(part, 'model', scatter_dimension=1, tiled=True, axis_ind...  71.2 us
    pallas_call x4, Pallas kernels, attend(): pl.pallas_call(kernel, out_shape=jax.ShapeDtypeStruct((2, rows, head_dim)...  45.4 us
  transfers between devices with their start and end apart: 69, of which 35 were waited for; matrix products, arithmetic and copies ran while one was open for 4% of the time, Pallas kernels for 29%

profile of v1, /device:TPU:97, one launch (start us, length us, event | category | flops | bytes accessed | tf_op | source)
XLA Modules:
  0.0 1562.1 jit_solution(549045514434799688)
XLA Ops:
  34.9 17.8 %collective-permute-done.1 = bf16[128,4096]{1,0:T(8,128)(2,1)S(1)} collective-permute-done((bf16[128,4096]{1,0:T(8,128)(2,1)S(1)}, bf16[128,4096]{1,0:T(8,128)(2,1)S(1)}, u32[]{:S(2)}, u32[]{:S(2)}) %collective-permute-start.1) | collective-permute-done | bytes 1048608 | tf_op jit(solution)/shard_map/ppermute | solution.py:236
  52.7 22.6 %collective-permute-done.11 = bf16[128,4096]{1,0:T(8,128)(2,1)} collective-permute-done((bf16[128,4096]{1,0:T(8,128)(2,1)S(1)}, bf16[128,4096]{1,0:T(8,128)(2,1)}, u32[]{:S(2)}, u32[]{:S(2)}) %collective-permute-start.11) | collective-permute-done | bytes 1048608 | tf_op jit(solution)/shard_map/ppermute | solution.py:236
  122.9 102.7 %collective-permute-done.4.refs_4_ = bf16[1024,2560]{1,0:T(8,128)(2,1)} collective-permute-done((bf16[1024,2560]{1,0:T(8,128)(2,1)}, bf16[1024,2560]{1,0:T(8,128)(2,1)}, u32[]{:S(2)}, u32[]{:S(2)}) %collective-permute-start.4) | collective-permute-done | bytes 5242912 | tf_op jit(solution)/shard_map/ppermute | solution.py:236
  237.3 54.5 %collective-permute-done.15.refs_4_ = bf16[1280,1024]{1,0:T(8,128)(2,1)} collective-permute-done((bf16[1280,1024]{1,0:T(8,128)(2,1)}, bf16[1280,1024]{1,0:T(8,128)(2,1)}, u32[]{:S(2)}, u32[]{:S(2)}) %collective-permute-start.15) | collective-permute-done | bytes 2621472 | tf_op jit(solution)/shard_map/ppermute | solution.py:236
  293.0 47.7 %collective-permute-done.5.refs_1_ = bf16[1024,2560]{1,0:T(8,128)(2,1)} collective-permute-done((bf16[1024,2560]{1,0:T(8,128)(2,1)}, bf16[1024,2560]{1,0:T(8,128)(2,1)}, u32[]{:S(2)}, u32[]{:S(2)}) %collective-permute-start.5) | collective-permute-done | bytes 5242912 | tf_op jit(solution)/shard_map/ppermute | solution.py:236
  342.6 43.8 %shard_map.68.refs_3_ = f32[2,1024,2560]{2,1,0:T(8,128)} custom-call(s32[3]{0:T(128)} %pad_add_fusion.1.ids_ref, bf16[1024,4096]{1,0:T(8,128)(2,1)} %all-gather.7.cloned.1.call-done.refs_0_.refs_1_.refs_2_, bf16[1024,4096]{1,0:T(8,128)(2,1)} %all-gather.7.cloned.1.call-done.refs_0_.refs_1_.refs_2_, ...), custom_call_target="tpu_custom_call" | custom-call | flops 32212254720 | bytes 48234496 | tf_op jit(solution)/shard_map/pallas_call | solution.py:65
  386.4 43.8 %shard_map.65.refs_3_ = f32[2,1024,2560]{2,1,0:T(8,128)} custom-call(s32[3]{0:T(128)} %pad_add_fusion.1.ids_ref, bf16[1024,4096]{1,0:T(8,128)(2,1)} %all-gather.5.cloned.1.call-done.refs_0_.refs_1_.refs_2_, bf16[1024,4096]{1,0:T(8,128)(2,1)} %all-gather.5.cloned.1.call-done.refs_0_.refs_1_.refs_2_, ...), custom_call_target="tpu_custom_call" | custom-call | flops 32212254720 | bytes 48234496 | tf_op jit(solution)/shard_map/pallas_call | solution.py:65
  430.2 22.2 %shard_map.69.q_ref.k_ref.v_ref = bf16[2,1024,2560]{2,1,0:T(8,128)(2,1)} custom-call(s32[1]{0:T(128)} %bitcast.1.ids_ref, bf16[1024,4096]{1,0:T(8,128)(2,1)} %all-gather.7.cloned.1.call-done.refs_0_.refs_1_.refs_2_, bf16[1024,2560]{1,0:T(8,128)(2,1)} %collective-permute-done.5.refs_1_, bf16[1024,2560]{1,0:T(8,128)(2,1)} %collective-permute-done.6.refs_2_, ...), custom_call_target="tpu_custom_call" | custom-call | flops 10737418240 | bytes 23068672 | tf_op jit(solution)/shard_map/pallas_call | solution.py:65
  463.8 22.2 %shard_map.66.q_ref.k_ref.v_ref = bf16[2,1024,2560]{2,1,0:T(8,128)(2,1)} custom-call(s32[1]{0:T(128)} %bitcast.1.ids_ref, bf16[1024,4096]{1,0:T(8,128)(2,1)} %all-gather.5.cloned.1.call-done.refs_0_.refs_1_.refs_2_, bf16[1024,2560]{1,0:T(8,128)(2,1)} %collective-permute-done.5.refs_1_, bf16[1024,2560]{1,0:T(8,128)(2,1)} %collective-permute-done.6.refs_2_, ...), custom_call_target="tpu_custom_call" | custom-call | flops 10737418240 | bytes 23068672 | tf_op jit(solution)/shard_map/pallas_call | solution.py:65
  509.2 17.4 %shard_map.73 = bf16[2,1024,1024]{2,1,0:T(8,128)(2,1)} custom-call(bf16[2,1024,256]{2,1,0:T(8,128)(2,1)} %shard_map.67.refs_0_, bf16[2,1024,1024]{2,1,0:T(8,128)(2,1)} %fusion.19.refs_1_, bf16[2,1024,256]{2,1,0:T(8,128)(2,1)} %shard_map.70.refs_2_, bf16[2,1024,1024]{2,1,0:T(8,128)(2,1)} %fusion.18.refs_3_, ...), custom_call_target="tpu_custom_call" | custom-call | flops 10737418240 | bytes 19922944 | tf_op jit(solution)/shard_map/pallas_call | solution.py:100
  531.9 17.5 %shard_map.72 = bf16[2,1024,1024]{2,1,0:T(8,128)(2,1)} custom-call(bf16[2,1024,256]{2,1,0:T(8,128)(2,1)} %shard_map.67.refs_0_, bf16[2,1024,1024]{2,1,0:T(8,128)(2,1)} %fusion.19.refs_1_, bf16[2,1024,256]{2,1,0:T(8,128)(2,1)} %shard_map.70.refs_2_, bf16[2,1024,1024]{2,1,0:T(8,128)(2,1)} %fusion.18.refs_3_, bf16[1280,1024]{1,0:T(8,128)(2,1)} %copy-done.7, ...), custom_call_target="tpu_custom_call" | custom-call | flops 10737418240 | bytes 19922944 | tf_op jit(solution)/shard_map/pallas_call | solution.py:100
  551.2 58.3 %collective-permute-done.23.refs_4_ = bf16[1280,1024]{1,0:T(8,128)(2,1)S(1)} collective-permute-done((bf16[1280,1024]{1,0:T(8,128)(2,1)}, bf16[1280,1024]{1,0:T(8,128)(2,1)S(1)}, u32[]{:S(2)}, u32[]{:S(2)}) %collective-permute-start.23) | collective-permute-done | bytes 2621472 | tf_op jit(solution)/shard_map/ppermute | solution.py:236
  635.2 57.7 %collective-permute-done.21.refs_4_ = bf16[1280,1024]{1,0:T(8,128)(2,1)S(1)} collective-permute-done((bf16[1280,1024]{1,0:T(8,128)(2,1)S(1)}, bf16[1280,1024]{1,0:T(8,128)(2,1)S(1)}, u32[]{:S(2)}, u32[]{:S(2)}) %collective-permute-start.21) | collective-permute-done | bytes 2621472 | tf_op jit(solution)/shard_map/ppermute | solution.py:236
  727.3 35.9 %reduce-scatter.13.cloned.1.call-done = bf16[2,256,1024]{2,1,0:T(8,128)(2,1)} async-done(((bf16[2,1024,1024]{2,1,0:T(8,128)(2,1)}), bf16[2,256,1024]{2,1,0:T(8,128)(2,1)}) %reduce-scatter.13.cloned.1.call-update) | async-done | bytes 1048592 | tf_op jit(solution)/shard_map/reduce_scatter | solution.py:296
  822.3 18.5 %collective-permute-done.39 = bf16[128,4096]{1,0:T(8,128)(2,1)S(1)} collective-permute-done((bf16[128,4096]{1,0:T(8,128)(2,1)S(1)}, bf16[128,4096]{1,0:T(8,128)(2,1)S(1)}, u32[]{:S(2)}, u32[]{:S(2)}) %collective-permute-start.39) | collective-permute-done | bytes 1048608 | tf_op jit(solution)/shard_map/ppermute | solution.py:236
  878.2 110.3 %collective-permute-done.32.refs_4_ = bf16[1024,2560]{1,0:T(8,128)(2,1)} collective-permute-done((bf16[1024,2560]{1,0:T(8,128)(2,1)}, bf16[1024,2560]{1,0:T(8,128)(2,1)}, u32[]{:S(2)}, u32[]{:S(2)}) %collective-permute-start.32) | collective-permute-done | bytes 5242912 | tf_op jit(solution)/shard_map/ppermute | solution.py:236
  1006.3 97.2 %collective-permute-done.33.refs_1_ = bf16[1024,2560]{1,0:T(8,128)(2,1)} collective-permute-done((bf16[1024,2560]{1,0:T(8,128)(2,1)}, bf16[1024,2560]{1,0:T(8,128)(2,1)}, u32[]{:S(2)}, u32[]{:S(2)}) %collective-permute-start.33) | collective-permute-done | bytes 5242912 | tf_op jit(solution)/shard_map/ppermute | solution.py:236
  1105.6 43.8 %shard_map.80.refs_3_ = f32[2,1024,2560]{2,1,0:T(8,128)} custom-call(s32[3]{0:T(128)} %pad_add_fusion.1.ids_ref, bf16[1024,4096]{1,0:T(8,128)(2,1)} %all-gather.11.cloned.1.call-done.refs_0_.refs_1_.refs_2_, bf16[1024,4096]{1,0:T(8,128)(2,1)} %all-gather.11.cloned.1.call-done.refs_0_.refs_1_.refs_2_, ...), custom_call_target="tpu_custom_call" | custom-call | flops 32212254720 | bytes 48234496 | tf_op jit(solution)/shard_map/pallas_call | solution.py:65
  1149.3 22.2 %shard_map.81.q_ref.k_ref.v_ref = bf16[2,1024,2560]{2,1,0:T(8,128)(2,1)} custom-call(s32[1]{0:T(128)} %bitcast.1.ids_ref, bf16[1024,4096]{1,0:T(8,128)(2,1)} %all-gather.11.cloned.1.call-done.refs_0_.refs_1_.refs_2_, bf16[1024,2560]{1,0:T(8,128)(2,1)} %collective-permute-done.33.refs_1_, bf16[1024,2560]{1,0:T(8,128)(2,1)} %collective-permute-done.34.refs_2_, ...), custom_call_target="tpu_custom_call" | custom-call | flops 10737418240 | bytes 23068672 | tf_op jit(solution)/shard_map/pallas_call | solution.py:65
  1182.9 43.8 %shard_map.77.refs_3_ = f32[2,1024,2560]{2,1,0:T(8,128)} custom-call(s32[3]{0:T(128)} %pad_add_fusion.1.ids_ref, bf16[1024,4096]{1,0:T(8,128)(2,1)} %all-gather.9.cloned.1.call-done.refs_0_.refs_1_.refs_2_, bf16[1024,4096]{1,0:T(8,128)(2,1)} %all-gather.9.cloned.1.call-done.refs_0_.refs_1_.refs_2_, ...), custom_call_target="tpu_custom_call" | custom-call | flops 32212254720 | bytes 48234496 | tf_op jit(solution)/shard_map/pallas_call | solution.py:65
  1226.7 22.2 %shard_map.78.q_ref.k_ref.v_ref = bf16[2,1024,2560]{2,1,0:T(8,128)(2,1)} custom-call(s32[1]{0:T(128)} %bitcast.1.ids_ref, bf16[1024,4096]{1,0:T(8,128)(2,1)} %all-gather.9.cloned.1.call-done.refs_0_.refs_1_.refs_2_, bf16[1024,2560]{1,0:T(8,128)(2,1)} %collective-permute-done.33.refs_1_, bf16[1024,2560]{1,0:T(8,128)(2,1)} %collective-permute-done.34.refs_2_, ...), custom_call_target="tpu_custom_call" | custom-call | flops 10737418240 | bytes 23068672 | tf_op jit(solution)/shard_map/pallas_call | solution.py:65
  1314.4 57.4 %collective-permute-done.51.refs_4_ = bf16[1280,1024]{1,0:T(8,128)(2,1)S(1)} collective-permute-done((bf16[1280,1024]{1,0:T(8,128)(2,1)}, bf16[1280,1024]{1,0:T(8,128)(2,1)S(1)}, u32[]{:S(2)}, u32[]{:S(2)}) %collective-permute-start.51) | collective-permute-done | bytes 2621472 | tf_op jit(solution)/shard_map/ppermute | solution.py:236
  1398.5 57.0 %collective-permute-done.49.refs_4_ = bf16[1280,1024]{1,0:T(8,128)(2,1)S(1)} collective-permute-done((bf16[1280,1024]{1,0:T(8,128)(2,1)S(1)}, bf16[1280,1024]{1,0:T(8,128)(2,1)S(1)}, u32[]{:S(2)}, u32[]{:S(2)}) %collective-permute-start.49) | collective-permute-done | bytes 2621472 | tf_op jit(solution)/shard_map/ppermute | solution.py:236
  1489.6 35.2 %reduce-scatter.21.cloned.1.call-done = bf16[2,256,1024]{2,1,0:T(8,128)(2,1)} async-done(((bf16[2,1024,1024]{2,1,0:T(8,128)(2,1)}), bf16[2,256,1024]{2,1,0:T(8,128)(2,1)}) %reduce-scatter.21.cloned.1.call-update) | async-done | bytes 1048592 | tf_op jit(solution)/shard_map/reduce_scatter | solution.py:296
  (251 shorter events, 475.9 us)
Async XLA Ops:
  6.5 336.0 %all-gather.7.cloned.1.call-start = ((), (), s32[]{:S(2)}) async-start(), calls=%async_computation.9 | async-start | bytes 10485760 | tf_op jit(solution)/shard_map/all_gather | solution.py:282
  81.5 304.9 %all-gather.5.cloned.1.call-start = ((), (), s32[]{:S(2)}) async-start(), calls=%async_computation.8 | async-start | bytes 10485760 | tf_op jit(solution)/shard_map/all_gather | solution.py:282
  110.9 114.7 %collective-permute-start.4 = (bf16[1024,2560]{1,0:T(8,128)(2,1)}, bf16[1024,2560]{1,0:T(8,128)(2,1)}, u32[]{:S(2)}, u32[]{:S(2)}) collective-permute-start(bf16[1024,2560]{1,0:T(8,128)(2,1)} %get-tuple-element.26), channel_id=1, source_target_pairs={{0,8},{1,9},{2,10},{3,11},{4,12},{5,13},{6,14},{7,15},{8,0},{9,1},... | collective-permute-start | bytes 15728648 | tf_op jit(solution)/shard_map/ppermute | solution.py:236
  110.9 117.2 %collective-permute-start.7 = (bf16[1024,2560]{1,0:T(8,128)(2,1)}, bf16[1024,2560]{1,0:T(8,128)(2,1)}, u32[]{:S(2)}, u32[]{:S(2)}) collective-permute-start(bf16[1024,2560]{1,0:T(8,128)(2,1)} %get-tuple-element.25.refs_3_), channel_id=1, source_target_pairs={{0,24},{1,25},{2,26},{3,27},{4,28},{5,29},{6,30},{7,31},{8,16},{9,... | collective-permute-start | bytes 15728648 | tf_op jit(solution)/shard_map/ppermute | solution.py:236
  115.0 604.0 %reduce-scatter.11.cloned.1.call-start = ((), (), s32[]{:S(2)}) async-start(), calls=%async_computation.11 | async-start | bytes 5242880 | tf_op jit(solution)/shard_map/reduce_scatter | solution.py:296
  225.6 115.1 %collective-permute-start.5 = (bf16[1024,2560]{1,0:T(8,128)(2,1)}, bf16[1024,2560]{1,0:T(8,128)(2,1)}, u32[]{:S(2)}, u32[]{:S(2)}) collective-permute-start(bf16[1024,2560]{1,0:T(8,128)(2,1)} %collective-permute-done.4.refs_4_), channel_id=1, source_target_pairs={{0,24},{1,25},{2,26},{3,27},{4,28},{5,29},{6,30},{7,31},{8,16},{9,... | collective-permute-start | bytes 15728648 | tf_op jit(solution)/shard_map/ppermute | solution.py:236
  227.0 115.5 %collective-permute-start.8 = (bf16[1024,2560]{1,0:T(8,128)(2,1)}, bf16[1024,2560]{1,0:T(8,128)(2,1)}, u32[]{:S(2)}, u32[]{:S(2)}) collective-permute-start(bf16[1024,2560]{1,0:T(8,128)(2,1)} %get-tuple-element.25.refs_3_), channel_id=1, source_target_pairs={{0,1},{1,0},{2,3},{3,2},{4,5},{5,4},{6,7},{7,6},{8,9},{9,8},{10,11... | collective-permute-start | bytes 15728648 | tf_op jit(solution)/shard_map/ppermute | solution.py:236
  228.1 114.5 %collective-permute-start.10 = (bf16[1024,2560]{1,0:T(8,128)(2,1)}, bf16[1024,2560]{1,0:T(8,128)(2,1)}, u32[]{:S(2)}, u32[]{:S(2)}) collective-permute-start(bf16[1024,2560]{1,0:T(8,128)(2,1)} %collective-permute-done.7.refs_5_), channel_id=1, source_target_pairs={{0,1},{1,0},{2,3},{3,2},{4,5},{5,4},{6,7},{7,6},{8,9},{9,8},{10,11... | collective-permute-start | bytes 15728648 | tf_op jit(solution)/shard_map/ppermute | solution.py:236
  228.1 114.5 %collective-permute-start.9 = (bf16[1024,2560]{1,0:T(8,128)(2,1)}, bf16[1024,2560]{1,0:T(8,128)(2,1)}, u32[]{:S(2)}, u32[]{:S(2)}) collective-permute-start(bf16[1024,2560]{1,0:T(8,128)(2,1)} %collective-permute-done.4.refs_4_), channel_id=1, source_target_pairs={{0,1},{1,0},{2,3},{3,2},{4,5},{5,4},{6,7},{7,6},{8,9},{9,8},{10,11... | collective-permute-start | bytes 15728648 | tf_op jit(solution)/shard_map/ppermute | solution.py:236
  291.8 217.4 %collective-permute-start.16 = (bf16[1280,1024]{1,0:T(8,128)(2,1)}, bf16[1280,1024]{1,0:T(8,128)(2,1)}, u32[]{:S(2)}, u32[]{:S(2)}) collective-permute-start(bf16[1280,1024]{1,0:T(8,128)(2,1)} %collective-permute-done.15.refs_4_), channel_id=1, source_target_pairs={{0,1},{1,0},{2,3},{3,2},{4,5},{5,4},{6,7},{7,6},{8,9},{9,8},{10,11... | collective-permute-start | bytes 7864328 | tf_op jit(solution)/shard_map/ppermute | solution.py:236
  526.7 192.4 %reduce-scatter.9.cloned.1.call-start = ((), (), s32[]{:S(2)}) async-start(), calls=%async_computation.10 | async-start | bytes 5242880 | tf_op jit(solution)/shard_map/reduce_scatter | solution.py:296
  549.5 177.8 %reduce-scatter.15.cloned.1.call-start = ((), (), s32[]{:S(2)}) async-start(), calls=%async_computation.13 | async-start | bytes 5242880 | tf_op jit(solution)/shard_map/reduce_scatter | solution.py:296
  632.1 131.2 %reduce-scatter.13.cloned.1.call-start = ((), (), s32[]{:S(2)}) async-start(), calls=%async_computation.12 | async-start | bytes 5242880 | tf_op jit(solution)/shard_map/reduce_scatter | solution.py:296
  718.9 386.6 %all-gather.11.cloned.1.call-start = ((), (), s32[]{:S(2)}) async-start(), calls=%async_computation.15 | async-start | bytes 10485760 | tf_op jit(solution)/shard_map/all_gather | solution.py:282
  844.7 338.2 %all-gather.9.cloned.1.call-start = ((), (), s32[]{:S(2)}) async-start(), calls=%async_computation.14 | async-start | bytes 10485760 | tf_op jit(solution)/shard_map/all_gather | solution.py:282
  873.8 114.7 %collective-permute-start.32 = (bf16[1024,2560]{1,0:T(8,128)(2,1)}, bf16[1024,2560]{1,0:T(8,128)(2,1)}, u32[]{:S(2)}, u32[]{:S(2)}) collective-permute-start(bf16[1024,2560]{1,0:T(8,128)(2,1)} %get-tuple-element.24), channel_id=1, source_target_pairs={{0,8},{1,9},{2,10},{3,11},{4,12},{5,13},{6,14},{7,15},{8,0},{9,1},... | collective-permute-start | bytes 15728648 | tf_op jit(solution)/shard_map/ppermute | solution.py:236
  874.2 125.0 %collective-permute-start.35 = (bf16[1024,2560]{1,0:T(8,128)(2,1)}, bf16[1024,2560]{1,0:T(8,128)(2,1)}, u32[]{:S(2)}, u32[]{:S(2)}) collective-permute-start(bf16[1024,2560]{1,0:T(8,128)(2,1)} %get-tuple-element.23.refs_3_), channel_id=1, source_target_pairs={{0,24},{1,25},{2,26},{3,27},{4,28},{5,29},{6,30},{7,31},{8,16},{9,... | collective-permute-start | bytes 15728648 | tf_op jit(solution)/shard_map/ppermute | solution.py:236
  878.1 603.2 %reduce-scatter.19.cloned.1.call-start = ((), (), s32[]{:S(2)}) async-start(), calls=%async_computation.17 | async-start | bytes 5242880 | tf_op jit(solution)/shard_map/reduce_scatter | solution.py:296
  988.5 115.0 %collective-permute-start.33 = (bf16[1024,2560]{1,0:T(8,128)(2,1)}, bf16[1024,2560]{1,0:T(8,128)(2,1)}, u32[]{:S(2)}, u32[]{:S(2)}) collective-permute-start(bf16[1024,2560]{1,0:T(8,128)(2,1)} %collective-permute-done.32.refs_4_), channel_id=1, source_target_pairs={{0,24},{1,25},{2,26},{3,27},{4,28},{5,29},{6,30},{7,31},{8,16},{9,... | collective-permute-start | bytes 15728648 | tf_op jit(solution)/shard_map/ppermute | solution.py:236
  998.8 106.7 %collective-permute-start.36 = (bf16[1024,2560]{1,0:T(8,128)(2,1)}, bf16[1024,2560]{1,0:T(8,128)(2,1)}, u32[]{:S(2)}, u32[]{:S(2)}) collective-permute-start(bf16[1024,2560]{1,0:T(8,128)(2,1)} %get-tuple-element.23.refs_3_), channel_id=1, source_target_pairs={{0,1},{1,0},{2,3},{3,2},{4,5},{5,4},{6,7},{7,6},{8,9},{9,8},{10,11... | collective-permute-start | bytes 15728648 | tf_op jit(solution)/shard_map/ppermute | solution.py:236
  1105.5 166.6 %collective-permute-start.44 = (bf16[1280,1024]{1,0:T(8,128)(2,1)}, bf16[1280,1024]{1,0:T(8,128)(2,1)}, u32[]{:S(2)}, u32[]{:S(2)}) collective-permute-start(bf16[1280,1024]{1,0:T(8,128)(2,1)} %collective-permute-done.43.refs_4_), channel_id=1, source_target_pairs={{0,1},{1,0},{2,3},{3,2},{4,5},{5,4},{6,7},{7,6},{8,9},{9,8},{10,11... | collective-permute-start | bytes 7864328 | tf_op jit(solution)/shard_map/ppermute | solution.py:236
  1289.5 191.8 %reduce-scatter.17.cloned.1.call-start = ((), (), s32[]{:S(2)}) async-start(), calls=%async_computation.16 | async-start | bytes 5242880 | tf_op jit(solution)/shard_map/reduce_scatter | solution.py:296
  1311.9 177.6 %reduce-scatter.23.cloned.1.call-start = ((), (), s32[]{:S(2)}) async-start(), calls=%async_computation.19 | async-start | bytes 5242880 | tf_op jit(solution)/shard_map/reduce_scatter | solution.py:296
  1394.5 130.3 %reduce-scatter.21.cloned.1.call-start = ((), (), s32[]{:S(2)}) async-start(), calls=%async_computation.18 | async-start | bytes 5242880 | tf_op jit(solution)/shard_map/reduce_scatter | solution.py:296
  (72 other events, 2649.3 us)
Sparse Core Ops, SparseCore 0:
  81.6 81.0 all-gather.6
  164.3 81.4 all-gather.4
  526.8 43.8 reduce-scatter.10
  572.9 43.9 reduce-scatter.8
  632.2 44.1 reduce-scatter.14
  719.1 44.1 reduce-scatter.12
  844.9 79.2 all-gather.10
  925.7 81.4 all-gather.8
  1289.6 42.9 reduce-scatter.18
  1334.8 44.0 reduce-scatter.16
  1394.6 43.3 reduce-scatter.22
  1481.4 43.3 reduce-scatter.20

commit v2 on v1

--- a/solution.py
+++ b/solution.py
@@ -8,14 +8,6 @@
 
 EPSILON = 1e-6
 BOTH = ('data', 'model')
-
-
-def layer_norm(act_in, gain_vec):
-    act_f32 = act_in.astype(jnp.float32)
-    row_mean = jnp.mean(act_f32, axis=-1, keepdims=True)
-    centered = act_f32 - row_mean
-    row_var = jnp.mean(centered * centered, axis=-1, keepdims=True)
-    return (centered * lax.rsqrt(row_var + EPSILON) * gain_vec.astype(jnp.float32)).astype(jnp.bfloat16)
 
 
 def matmul(lhs, rhs):
@@ -70,41 +62,40 @@
     )(jnp.stack(slab_ids).astype(jnp.int32), *args)
 
 
-def mix_out(attn, mlp, w_ours, w_theirs):
-    n_seq = len(attn)
-    _, rows, q_cut = attn[0].shape
-    ff = mlp[0].shape[2]
-    cols = w_ours.shape[1]
-    chunk = 512
-    steps = rows // chunk
-
-    def kernel(*refs):
-        lhs, (wa_ref, wb_ref, out_ref) = refs[:-3], refs[-3:]
-
-        def run(a_ref, m_ref):
-            total = matmul(a_ref[0], wa_ref[:q_cut, :]) + matmul(m_ref[0], wa_ref[q_cut:, :])
-            total = total + matmul(a_ref[1], wb_ref[:q_cut, :]) + matmul(m_ref[1], wb_ref[q_cut:, :])
-            out_ref[0] = total.astype(jnp.bfloat16)
-
-        for b in range(n_seq):
-            @pl.when(pl.program_id(0) == b)
-            def _(b=b):
-                run(lhs[2 * b], lhs[2 * b + 1])
-
-    in_specs, args = [], []
-    for b in range(n_seq):
-        for arr in (attn[b], mlp[b]):
-            in_specs.append(pl.BlockSpec((2, chunk, arr.shape[2]), lambda s, m, b=b: (0, jnp.where(s == b, m, jnp.where(s < b, 0, steps - 1)), 0)))
-            args.append(arr)
-    in_specs += [pl.BlockSpec(w_ours.shape, lambda s, m: (0, 0))] * 2
-    return pl.pallas_call(
-        kernel,
-        out_shape=jax.ShapeDtypeStruct((n_seq, rows, cols), jnp.bfloat16),
-        grid=(n_seq, steps),
-        in_specs=in_specs,
-        out_specs=pl.BlockSpec((1, chunk, cols), lambda s, m: (s, m, 0)),
-        cost_estimate=pl.CostEstimate(flops=4 * n_seq * rows * (q_cut + ff) * cols, bytes_accessed=4 * n_seq * rows * (q_cut + ff) + 4 * w_ours.size + 2 * n_seq * rows * cols, transcendentals=0),
-    )(*args, w_ours, w_theirs)
+def mix_out(attn, mlp, ours, theirs):
+    _, rows, q_cut = attn.shape
+    ff = mlp.shape[2]
+    n_slabs = len(ours)
+    depth, cols = ours[0].shape
+    tile, chunk = 512, 512
+    tiles = cols // tile
+
+    def kernel(a_ref, m_ref, *refs):
+        w_refs, out_ref = refs[:-1], refs[-1]
+        for i in range(n_slabs):
+            @pl.when(pl.program_id(0) == i)
+            def _(i=i):
+                wa_ref, wb_ref = w_refs[i], w_refs[n_slabs + i]
+
+                @pl.loop(0, rows // chunk)
+                def _(step):
+                    at = pl.ds(pl.multiple_of(step * chunk, chunk), chunk)
+                    total = matmul(m_ref[0, at, :], wa_ref[q_cut:, :]) + matmul(m_ref[1, at, :], wb_ref[q_cut:, :])
+                    total = total + matmul(a_ref[0, at, :], wa_ref[:q_cut, :]) + matmul(a_ref[1, at, :], wb_ref[:q_cut, :])
+                    out_ref[at, :] = total.astype(jnp.bfloat16)
+
+    def w_spec(i):
+        return pl.BlockSpec((depth, tile), lambda s, n: (0, jnp.where(s == i, n, jnp.where(s < i, 0, tiles - 1))))
+
+    w_specs = [w_spec(i) for i in range(n_slabs)] * 2
+    return pl.pallas_call(
+        kernel,
+        out_shape=jax.ShapeDtypeStruct((rows, n_slabs * cols), jnp.bfloat16),
+        grid=(n_slabs, tiles),
+        in_specs=[pl.BlockSpec(attn.shape, lambda s, n: (0, 0, 0)), pl.BlockSpec(mlp.shape, lambda s, n: (0, 0, 0))] + w_specs,
+        out_specs=pl.BlockSpec((rows, tile), lambda s, n: (0, s * tiles + n)),
+        cost_estimate=pl.CostEstimate(flops=4 * n_slabs * rows * (q_cut + ff) * cols, bytes_accessed=4 * rows * (q_cut + ff) + 4 * n_slabs * depth * cols + 2 * n_slabs * rows * cols, transcendentals=0),
+    )(attn, mlp, *ours, *theirs)
 
 
 def attend(both, core, key_len, head_dim):
@@ -112,16 +103,19 @@
     chunk = 256
 
     def kernel(nums_ref, q_ref, k_ref, v_ref, out_ref):
-        start = pl.program_id(1) * chunk
-        scores = lax.dot_general(q_ref[0], k_ref[0], (((1,), (1,)), ((), ())), preferred_element_type=jnp.float32) * head_dim ** -0.5
-        q_pos = start + lax.broadcasted_iota(jnp.int32, scores.shape, 0)
-        k_pos = lax.broadcasted_iota(jnp.int32, scores.shape, 1)
-        scores = jnp.where((k_pos <= q_pos) & (k_pos < nums_ref[1]), scores, -1e30)
-        weights = jnp.exp(scores - jnp.max(scores, axis=-1, keepdims=True))
-        norm = jnp.sum(weights, axis=-1, keepdims=True)
-        probs = weights / norm
-        out = jnp.dot(probs, v_ref[0].astype(jnp.float32), preferred_element_type=jnp.float32)
-        out_ref[0] = out.astype(jnp.bfloat16)
+        for step in range(rows // chunk):
+            @pl.when(pl.program_id(1) == step)
+            def _(step=step):
+                seen = (step + 1) * chunk
+                scores = lax.dot_general(q_ref[0], k_ref[0, :seen, :], (((1,), (1,)), ((), ())), preferred_element_type=jnp.float32) * head_dim ** -0.5
+                q_pos = step * chunk + lax.broadcasted_iota(jnp.int32, scores.shape, 0)
+                k_pos = lax.broadcasted_iota(jnp.int32, scores.shape, 1)
+                scores = jnp.where((k_pos <= q_pos) & (k_pos < nums_ref[1]), scores, -1e30)
+                weights = jnp.exp(scores - jnp.max(scores, axis=-1, keepdims=True))
+                norm = jnp.sum(weights, axis=-1, keepdims=True)
+                probs = weights / norm
+                out = jnp.dot(probs, v_ref[0, :seen, :].astype(jnp.float32), preferred_element_type=jnp.float32)
+                out_ref[0] = out.astype(jnp.bfloat16)
 
     return pl.pallas_call(
         kernel,
@@ -138,6 +132,118 @@
         ),
         cost_estimate=pl.CostEstimate(flops=8 * rows * rows * head_dim, bytes_accessed=16 * rows * head_dim, transcendentals=2 * rows * rows),
     )(jnp.stack([core, key_len]).astype(jnp.int32), both, both, both)
+
+
+def normalize(act_f32, gain_row):
+    row_mean = jnp.mean(act_f32, axis=-1, keepdims=True)
+    centered = act_f32 - row_mean
+    row_var = jnp.mean(centered * centered, axis=-1, keepdims=True)
+    return (centered * lax.rsqrt(row_var + EPSILON) * gain_row).astype(jnp.bfloat16)
+
+
+def pair_norm(mine, got_a, got_b, gain, core):
+    rows, width = mine.shape
+
+    def kernel(core_ref, mine_ref, a_ref, b_ref, gain_ref, out_ref, norm_ref):
+        def emit(at, src_ref):
+            val = src_ref[...]
+            out_ref[at, :] = val
+            norm_ref[at, :] = normalize(val.astype(jnp.float32), gain_ref[...].astype(jnp.float32))
+
+        top, bottom = pl.ds(0, rows), pl.ds(rows, rows)
+
+        @pl.when(core_ref[0] == 0)
+        def _():
+            emit(top, mine_ref)
+            emit(bottom, a_ref)
+
+        @pl.when(core_ref[0] == 1)
+        def _():
+            emit(top, a_ref)
+            emit(bottom, b_ref)
+
+    block = pl.BlockSpec((rows, width), lambda i, c: (0, 0))
+    out = pl.BlockSpec((2 * rows, width), lambda i, c: (0, 0))
+    return pl.pallas_call(
+        kernel,
+        out_shape=[jax.ShapeDtypeStruct((2 * rows, width), jnp.bfloat16)] * 2,
+        grid_spec=pltpu.PrefetchScalarGridSpec(
+            num_scalar_prefetch=1,
+            grid=(1,),
+            in_specs=[block, block, block, pl.BlockSpec((1, width), lambda i, c: (0, 0))],
+            out_specs=[out, out],
+        ),
+        cost_estimate=pl.CostEstimate(flops=40 * rows * width, bytes_accessed=14 * rows * width, transcendentals=rows),
+    )(core.reshape(1).astype(jnp.int32), mine, got_a, got_b, gain.reshape(1, width))
+
+
+def join_norm(hidden, pairs, others, gain, slab_ids):
+    rows, width = hidden.shape
+    n_parts = len(pairs)
+    slab = width // len(slab_ids)
+    chunk = rows // 2
+
+    def kernel(ids_ref, hid_ref, gain_ref, *refs):
+        p_refs, o_refs, (out_ref, norm_ref) = refs[:n_parts], refs[n_parts:2 * n_parts], refs[2 * n_parts:]
+        for i in range(len(slab_ids)):
+            at = pl.ds(pl.multiple_of(ids_ref[i] * slab, slab), slab)
+            ours = p_refs[i // 2][:, (i % 2) * slab:(i % 2 + 1) * slab].astype(jnp.float32)
+            theirs = o_refs[i // 2][:, (1 - i % 2) * slab:(2 - i % 2) * slab].astype(jnp.float32)
+            out_ref[:, at] = (hid_ref[:, at].astype(jnp.float32) + (ours + theirs)).astype(jnp.bfloat16)
+        norm_ref[...] = normalize(out_ref[...].astype(jnp.float32), gain_ref[...].astype(jnp.float32))
+
+    wide = pl.BlockSpec((chunk, width), lambda i, ids: (i, 0))
+    part = pl.BlockSpec((chunk, 2 * slab), lambda i, ids: (i, 0))
+    return pl.pallas_call(
+        kernel,
+        out_shape=[jax.ShapeDtypeStruct((rows, width), jnp.bfloat16)] * 2,
+        grid_spec=pltpu.PrefetchScalarGridSpec(
+            num_scalar_prefetch=1,
+            grid=(rows // chunk,),
+            in_specs=[wide, pl.BlockSpec((1, width), lambda i, ids: (0, 0))] + [part] * (2 * n_parts),
+            out_specs=[wide, wide],
+        ),
+        cost_estimate=pl.CostEstimate(flops=20 * rows * width, bytes_accessed=10 * rows * width, transcendentals=rows),
+    )(jnp.stack(slab_ids).astype(jnp.int32), hidden, gain.reshape(1, width), *pairs, *others)
+
+
+def finish(hidden, residuals, pairs, got_a, got_b, slab_ids, core):
+    n_seq = len(hidden)
+    rows, width = residuals[0].shape
+    slab = width // len(slab_ids)
+    n_parts = len(slab_ids) // 2
+
+    def kernel(nums_ref, *refs):
+        out_ref = refs[-1]
+        even = nums_ref[len(slab_ids)] == 0
+        per = 2 + 3 * n_parts
+        for b in range(n_seq):
+            mine = refs[per * b:per * (b + 1)]
+            hid_ref, res_ref, p_refs = mine[0], mine[1], mine[2:2 + n_parts]
+            a_refs, b_refs = mine[2 + n_parts:2 + 2 * n_parts], mine[2 + 2 * n_parts:]
+            for i in range(len(slab_ids)):
+                at = pl.ds(pl.multiple_of(nums_ref[i] * slab, slab), slab)
+                cut = slice((i % 2) * slab, (i % 2 + 1) * slab)
+                base = jnp.where(even, hid_ref[:, at].astype(jnp.float32), res_ref[:, at].astype(jnp.float32))
+                kept = jnp.where(even, p_refs[i // 2][:, cut].astype(jnp.float32), b_refs[i // 2][:, cut].astype(jnp.float32))
+                out_ref[b, :, at] = (base + (kept + a_refs[i // 2][:, cut].astype(jnp.float32))).astype(jnp.bfloat16)
+
+    wide = pl.BlockSpec((rows, width), lambda i, n: (0, 0))
+    part = pl.BlockSpec((rows, 2 * slab), lambda i, n: (0, 0))
+    args = []
+    for b in range(n_seq):
+        args += [hidden[b], residuals[b], *pairs[b], *got_a[b], *got_b[b]]
+    return pl.pallas_call(
+        kernel,
+        out_shape=jax.ShapeDtypeStruct((n_seq, rows, width), jnp.bfloat16),
+        grid_spec=pltpu.PrefetchScalarGridSpec(
+            num_scalar_prefetch=1,
+            grid=(1,),
+            in_specs=([wide, wide] + [part] * (3 * n_parts)) * n_seq,
+            out_specs=pl.BlockSpec((n_seq, rows, width), lambda i, n: (0, 0, 0)),
+        ),
+        cost_estimate=pl.CostEstimate(flops=8 * n_seq * rows * width, bytes_accessed=14 * n_seq * rows * width, transcendentals=0),
+    )(jnp.stack([*slab_ids, core]).astype(jnp.int32), *args)
 
 
 def split_columns(w_in, layer_idx, core, head_dim, q_group, ff_half):
@@ -230,6 +336,7 @@
     spread_a = table(lambda r, m: (r ^ 1, m ^ 1) if m % 2 == 0 else (r, m ^ 1))
     spread_b = table(lambda r, m: None if m % 2 == 0 else (r ^ 1, m))
     collect_a = table(lambda r, m: (r, m ^ 1) if m % 2 == 0 else (r ^ 1, m ^ 1))
+    cross = table(lambda r, m: (r ^ 1, m ^ 1))
     lanes = [list(range(0, n_model, 2)), list(range(1, n_model, 2))]
 
     def send(val, pairs):
@@ -264,47 +371,64 @@
             theirs = tuple(send(p, core_swap) for p in ours)
             return ours, theirs
 
-        hidden = x_loc
         w_pieces = []
         for layer_idx in range(n_layers):
             ins = pieces(*split_columns(w_in_loc, layer_idx, core, head_dim, q_group, ff_half))
             outs = pieces(*split_rows(w_attn_loc, w_mlp_loc, layer_idx, core))
             w_pieces.append((ins, outs))
 
+        hidden, normed = [], []
+        for b in range(batch_loc):
+            mine = x_loc[b]
+            got_a = send(mine, spread_a)
+            got_b = send(mine, spread_b)
+            hid, norm = pair_norm(mine, got_a, got_b, gain_all[0], core)
+            hidden.append(hid)
+            normed.append(norm)
+
+        def swap_slabs(val):
+            return jnp.concatenate([val[:, slab:], val[:, :slab]], axis=1)
+
+        ends = ([], [], [], [])
         for layer_idx in range(n_layers):
             ins, outs = w_pieces[layer_idx]
-            normed = layer_norm(hidden, gain_all[layer_idx])
-            h_seqs = []
+            is_last = layer_idx == n_layers - 1
+            h_seqs = [lax.all_gather(n, 'model', axis=0, tiled=True, axis_index_groups=lanes) for n in normed]
+            normed = []
+            totals = []
             for b in range(batch_loc):
-                got_a = send(normed[b], spread_a)
-                got_b = send(normed[b], spread_b)
-                pair = jnp.concatenate([jnp.where(even, normed[b], got_a), jnp.where(even, got_a, got_b)], axis=0)
-                h_seqs.append(lax.all_gather(pair, 'model', axis=0, tiled=True, axis_index_groups=lanes))
-            firsts_in, totals = (ins[0][:3], ins[1][:3]), []
+                if layer_idx == 0:
+                    totals.append(project(h_seqs[b], slabs[:3], ins[0][:3], ins[1][:3], None, False))
+            new_hidden = []
             for b in range(batch_loc):
-                totals.append(project(h_seqs[b], slabs[:3], *firsts_in, None, False))
-            attn_all, mlp_all = [], []
-            for b in range(batch_loc):
-                both = project(h_seqs[b], slabs[3:], ins[0][3:], ins[1][3:], totals[b], True)
+                if layer_idx == 0:
+                    both = project(h_seqs[b], slabs[3:], ins[0][3:], ins[1][3:], totals[b], True)
+                else:
+                    both = project(h_seqs[b], slabs, ins[0], ins[1], None, True)
                 ff_at = attn_width // 2 + head_dim
-                attn_all.append(attend(both, core, work_lens[b], head_dim))
+                attn = attend(both, core, work_lens[b], head_dim)
                 gate, up = both[:, :, ff_at:ff_at + ff_half], both[:, :, ff_at + ff_half:]
-                mlp_all.append((jax.nn.silu(gate.astype(jnp.float32)) * up.astype(jnp.float32)).astype(jnp.bfloat16))
-            firsts, seconds = [], []
-            for i in range(n_data):
-                part = mix_out(attn_all, mlp_all, outs[0][i], outs[1][i])
-                pair = lax.psum_scatter(part, 'model', scatter_dimension=1, tiled=True, axis_index_groups=lanes)
-                firsts.append(pair[:, :seq_loc])
-                seconds.append(pair[:, seq_loc:])
-            z_slabs = []
-            for i in range(n_data):
-                got_a = send(jnp.where(even, seconds[i], firsts[i ^ 1]), collect_a)
-                got_b = send(seconds[i ^ 1], spread_b)
-                z_slabs.append(jnp.where(even, firsts[i], got_b).astype(jnp.float32) + got_a.astype(jnp.float32))
-            z_loc = jnp.zeros(hidden.shape, jnp.float32)
-            for s, z in zip(slabs, z_slabs):
-                z_loc = lax.dynamic_update_slice_in_dim(z_loc, z, s * slab, axis=2)
-            hidden = (hidden.astype(jnp.float32) + z_loc).astype(jnp.bfloat16)
-        return hidden
+                mlp = (jax.nn.silu(gate.astype(jnp.float32)) * up.astype(jnp.float32)).astype(jnp.bfloat16)
+                pairs, got_a, got_b, others = [], [], [], []
+                for s in range(2):
+                    part = mix_out(attn, mlp, outs[0][2 * s:2 * s + 2], outs[1][2 * s:2 * s + 2])
+                    pair = lax.psum_scatter(part, 'model', scatter_dimension=0, tiled=True, axis_index_groups=lanes)
+                    pairs.append(pair)
+                    if is_last:
+                        first, second = pair[:seq_loc], pair[seq_loc:]
+                        got_a.append(send(jnp.where(even, second, swap_slabs(first)), collect_a))
+                        got_b.append(send(swap_slabs(second), spread_b))
+                    else:
+                        others.append(send(pair, cross))
+                if is_last:
+                    for kept, val in zip(ends, (send(hidden[b][seq_loc:], core_swap), pairs, got_a, got_b)):
+                        kept.append(val)
+                else:
+                    hid, norm = join_norm(hidden[b], pairs, others, gain_all[layer_idx + 1], slabs)
+                    new_hidden.append(hid)
+                    normed.append(norm)
+            if not is_last:
+                hidden = new_hidden
+        return finish(hidden, *ends, slabs, core)
 
     return jax.shard_map(two_layers, mesh=mesh, in_specs=(P(batch_axes, 'model', None), P(batch_axes), P(None, 'data'), P(None, 'data', 'model'), P(None, 'model', 'data'), P(None, 'model', 'data')), out_specs=P(batch_axes, 'model', None), check_vma=False)

time: 1570 us -> 1500 us (0.955)
  waiting for transfers between devices: 884 us -> 816 us
    ppermute x57 -> x51, waiting for transfers between devices: 812 us -> 762 us  [send(): return lax.ppermute(val, BOTH, pairs)]
    pallas_call x8 -> x13, Pallas kernels: 137 us -> 173 us  [the longest x8 141 us: mix_out(): pl.pallas_call(kernel, out_shape=jax.ShapeDtypeStruct((rows, n_slabs * co...]
    pallas_call x8 -> x6, Pallas kernels: 264 us -> 244 us  [project(): pl.pallas_call(kernel, out_shape=out_shape, grid_spec=pltpu.PrefetchScala...]
    reduce_scatter x8, waiting for transfers between devices: 71.2 us -> 53.9 us  [two_layers(): lax.psum_scatter(part, 'model', scatter_dimension=0, tiled=True, axis_ind...]
    ppermute x57 -> x51, starting transfers between devices: 71.4 us -> 58.2 us  [send(): return lax.ppermute(val, BOTH, pairs)]
  transfers between devices with their start and end apart: 69 -> 63, of which waited for: 35 -> 24; matrix products, arithmetic and copies ran while one was open for 4% -> 5% of each run, Pallas kernels for 29% -> 33%
where the time goes in v2:
time: 1500 us; the launch traced here: 1490 us
  waiting for transfers between devices  816 us (54%)
  Pallas kernels  492 us (33%)
  other arithmetic  66.5 us (4%)
  starting transfers between devices  60 us (4%)
  local copies, waits for them, and re-layouts  21.4 us (1%)
  blocking collectives  16.6 us (1%)
    ppermute x51, waiting for transfers between devices, send(): return lax.ppermute(val, BOTH, pairs)  762 us
    pallas_call x6, Pallas kernels, project(): pl.pallas_call(kernel, out_shape=out_shape, grid_spec=pltpu.PrefetchScala...  244 us
    pallas_call x8, Pallas kernels, mix_out(): pl.pallas_call(kernel, out_shape=jax.ShapeDtypeStruct((rows, n_slabs * co...  141 us
    ppermute x51, starting transfers between devices, send(): return lax.ppermute(val, BOTH, pairs)  58.2 us
    reduce_scatter x8, waiting for transfers between devices, two_layers(): lax.psum_scatter(part, 'model', scatter_dimension=0, tiled=True, axis_ind...  53.9 us
    pallas_call x4, Pallas kernels, attend(): pl.pallas_call(kernel, out_shape=jax.ShapeDtypeStruct((2, rows, head_dim)...  38.9 us
  transfers between devices with their start and end apart: 63, of which 24 were waited for; matrix products, arithmetic and copies ran while one was open for 5% of the time, Pallas kernels for 33%

profile of v2, /device:TPU:97, one launch (start us, length us, event | category | flops | bytes accessed | tf_op | source)
XLA Modules:
  0.0 1486.9 jit_solution(3075309234499223075)
XLA Ops:
  60.1 111.6 %collective-permute-done.4.refs_4_ = bf16[1024,2560]{1,0:T(8,128)(2,1)} collective-permute-done((bf16[1024,2560]{1,0:T(8,128)(2,1)}, bf16[1024,2560]{1,0:T(8,128)(2,1)}, u32[]{:S(2)}, u32[]{:S(2)}) %collective-permute-start.4) | collective-permute-done | bytes 5242912 | tf_op jit(solution)/shard_map/ppermute | solution.py:343
  213.2 73.2 %collective-permute-done.5.refs_1_ = bf16[1024,2560]{1,0:T(8,128)(2,1)} collective-permute-done((bf16[1024,2560]{1,0:T(8,128)(2,1)}, bf16[1024,2560]{1,0:T(8,128)(2,1)}, u32[]{:S(2)}, u32[]{:S(2)}) %collective-permute-start.5) | collective-permute-done | bytes 5242912 | tf_op jit(solution)/shard_map/ppermute | solution.py:343
  291.8 43.8 %shard_map.66.refs_3_ = f32[2,1024,2560]{2,1,0:T(8,128)} custom-call(s32[3]{0:T(128)} %pad_add_fusion.2.ids_ref, bf16[1024,4096]{1,0:T(8,128)(2,1)} %all-gather.5.cloned.1.call-done.refs_0_.refs_1_.refs_2_, bf16[1024,4096]{1,0:T(8,128)(2,1)} %all-gather.5.cloned.1.call-done.refs_0_.refs_1_.refs_2_, ...), custom_call_target="tpu_custom_call" | custom-call | flops 32212254720 | bytes 48234496 | tf_op jit(solution)/shard_map/pallas_call | solution.py:57
  335.6 22.2 %shard_map.67.q_ref.k_ref.v_ref = bf16[2,1024,2560]{2,1,0:T(8,128)(2,1)} custom-call(s32[1]{0:T(128)} %bitcast.3.ids_ref, bf16[1024,4096]{1,0:T(8,128)(2,1)} %all-gather.5.cloned.1.call-done.refs_0_.refs_1_.refs_2_, bf16[1024,2560]{1,0:T(8,128)(2,1)} %collective-permute-done.5.refs_1_, bf16[1024,2560]{1,0:T(8,128)(2,1)} %collective-permute-done.6.refs_2_, ...), custom_call_target="tpu_custom_call" | custom-call | flops 10737418240 | bytes 23068672 | tf_op jit(solution)/shard_map/pallas_call | solution.py:57
  375.2 17.6 %shard_map.70 = bf16[1024,2048]{1,0:T(8,128)(2,1)} custom-call(bf16[2,1024,256]{2,1,0:T(8,128)(2,1)} %shard_map.68.a_ref, bf16[2,1024,1024]{2,1,0:T(8,128)(2,1)} %fusion.19.m_ref, bf16[1280,1024]{1,0:T(8,128)(2,1)} %get-tuple-element.44.refs_0_, bf16[1280,1024]{1,0:T(8,128)(2,1)} %collective-permute-done.12.refs_1_, bf16[1280,1024]{1,0:T(8,128)(2,1)} %copy-done.15, ...), custom_call_target="tpu_custom_call" | custom-call | flops 10737418240 | bytes 19922944 | tf_op jit(solution)/shard_map/pallas_call | solution.py:91
  395.8 57.0 %collective-permute-done.15.refs_0_ = bf16[1280,1024]{1,0:T(8,128)(2,1)S(1)} collective-permute-done((bf16[1280,1024]{1,0:T(8,128)(2,1)}, bf16[1280,1024]{1,0:T(8,128)(2,1)S(1)}, u32[]{:S(2)}, u32[]{:S(2)}) %collective-permute-start.15) | collective-permute-done | bytes 2621472 | tf_op jit(solution)/shard_map/ppermute | solution.py:343
  454.3 54.7 %collective-permute-done.16.refs_1_ = bf16[1280,1024]{1,0:T(8,128)(2,1)S(1)} collective-permute-done((bf16[1280,1024]{1,0:T(8,128)(2,1)}, bf16[1280,1024]{1,0:T(8,128)(2,1)S(1)}, u32[]{:S(2)}, u32[]{:S(2)}) %collective-permute-start.16) | collective-permute-done | bytes 2621472 | tf_op jit(solution)/shard_map/ppermute | solution.py:343
  514.6 17.6 %shard_map.71 = bf16[1024,2048]{1,0:T(8,128)(2,1)} custom-call(bf16[2,1024,256]{2,1,0:T(8,128)(2,1)} %shard_map.68.a_ref, bf16[2,1024,1024]{2,1,0:T(8,128)(2,1)} %fusion.19.m_ref, bf16[1280,1024]{1,0:T(8,128)(2,1)} %copy-done.17, bf16[1280,1024]{1,0:T(8,128)(2,1)} %copy-done.18, bf16[1280,1024]{1,0:T(8,128)(2,1)} %copy-done.21, ...), custom_call_target="tpu_custom_call" | custom-call | flops 10737418240 | bytes 19922944 | tf_op jit(solution)/shard_map/pallas_call | solution.py:91
  534.0 43.7 %shard_map.80.refs_3_ = f32[2,1024,2560]{2,1,0:T(8,128)} custom-call(s32[3]{0:T(128)} %pad_add_fusion.2.ids_ref, bf16[1024,4096]{1,0:T(8,128)(2,1)} %all-gather.9.cloned.1.call-done.refs_0_.refs_1_.refs_2_, bf16[1024,4096]{1,0:T(8,128)(2,1)} %all-gather.9.cloned.1.call-done.refs_0_.refs_1_.refs_2_, ...), custom_call_target="tpu_custom_call" | custom-call | flops 32212254720 | bytes 48234496 | tf_op jit(solution)/shard_map/pallas_call | solution.py:57
  577.7 22.2 %shard_map.81.q_ref.k_ref.v_ref = bf16[2,1024,2560]{2,1,0:T(8,128)(2,1)} custom-call(s32[1]{0:T(128)} %bitcast.3.ids_ref, bf16[1024,4096]{1,0:T(8,128)(2,1)} %all-gather.9.cloned.1.call-done.refs_0_.refs_1_.refs_2_, bf16[1024,2560]{1,0:T(8,128)(2,1)} %collective-permute-done.5.refs_1_, bf16[1024,2560]{1,0:T(8,128)(2,1)} %collective-permute-done.6.refs_2_, ...), custom_call_target="tpu_custom_call" | custom-call | flops 10737418240 | bytes 23068672 | tf_op jit(solution)/shard_map/pallas_call | solution.py:57
  615.9 17.7 %shard_map.83 = bf16[1024,2048]{1,0:T(8,128)(2,1)} custom-call(bf16[2,1024,256]{2,1,0:T(8,128)(2,1)} %shard_map.82.a_ref, bf16[2,1024,1024]{2,1,0:T(8,128)(2,1)} %fusion.17.m_ref, bf16[1280,1024]{1,0:T(8,128)(2,1)} %get-tuple-element.44.refs_0_, bf16[1280,1024]{1,0:T(8,128)(2,1)} %collective-permute-done.12.refs_1_, bf16[1280,1024]{1,0:T(8,128)(2,1)} %copy-done.15, ...), custom_call_target="tpu_custom_call" | custom-call | flops 10737418240 | bytes 19922944 | tf_op jit(solution)/shard_map/pallas_call | solution.py:91
  665.4 23.6 %collective-permute-done.19.refs_2_ = bf16[256,2048]{1,0:T(8,128)(2,1)S(1)} collective-permute-done((bf16[256,2048]{1,0:T(8,128)(2,1)}, bf16[256,2048]{1,0:T(8,128)(2,1)S(1)}, u32[]{:S(2)}, u32[]{:S(2)}) %collective-permute-start.19) | collective-permute-done | bytes 1048608 | tf_op jit(solution)/shard_map/ppermute | solution.py:343
  689.0 22.0 %collective-permute-done.20.refs_3_ = bf16[256,2048]{1,0:T(8,128)(2,1)S(1)} collective-permute-done((bf16[256,2048]{1,0:T(8,128)(2,1)}, bf16[256,2048]{1,0:T(8,128)(2,1)S(1)}, u32[]{:S(2)}, u32[]{:S(2)}) %collective-permute-start.20) | collective-permute-done | bytes 1048608 | tf_op jit(solution)/shard_map/ppermute | solution.py:343
  730.6 112.6 %collective-permute-done.23.refs_5_ = bf16[1024,2560]{1,0:T(8,128)(2,1)} collective-permute-done((bf16[1024,2560]{1,0:T(8,128)(2,1)}, bf16[1024,2560]{1,0:T(8,128)(2,1)}, u32[]{:S(2)}, u32[]{:S(2)}) %collective-permute-start.23) | collective-permute-done | bytes 5242912 | tf_op jit(solution)/shard_map/ppermute | solution.py:343
  871.8 22.5 %collective-permute-done.45.refs_3_ = bf16[256,2048]{1,0:T(8,128)(2,1)} collective-permute-done((bf16[256,2048]{1,0:T(8,128)(2,1)}, bf16[256,2048]{1,0:T(8,128)(2,1)}, u32[]{:S(2)}, u32[]{:S(2)}) %collective-permute-start.45) | collective-permute-done | bytes 1048608 | tf_op jit(solution)/shard_map/ppermute | solution.py:343
  902.4 56.4 %collective-permute-done.25.refs_7_ = bf16[1024,2560]{1,0:T(8,128)(2,1)} collective-permute-done((bf16[1024,2560]{1,0:T(8,128)(2,1)}, bf16[1024,2560]{1,0:T(8,128)(2,1)}, u32[]{:S(2)}, u32[]{:S(2)}) %collective-permute-start.25) | collective-permute-done | bytes 5242912 | tf_op jit(solution)/shard_map/ppermute | solution.py:343
  963.8 58.5 %collective-permute-done.31.refs_1_ = bf16[1280,1024]{1,0:T(8,128)(2,1)} collective-permute-done((bf16[1280,1024]{1,0:T(8,128)(2,1)S(1)}, bf16[1280,1024]{1,0:T(8,128)(2,1)}, u32[]{:S(2)}, u32[]{:S(2)}) %collective-permute-start.31) | collective-permute-done | bytes 2621472 | tf_op jit(solution)/shard_map/ppermute | solution.py:343
  1023.2 55.9 %shard_map.74.q_ref.k_ref.v_ref = bf16[2,1024,2560]{2,1,0:T(8,128)(2,1)} custom-call(s32[4]{0:T(128)} %pad_add_fusion.ids_ref, bf16[1024,4096]{1,0:T(8,128)(2,1)} %all-gather.7.cloned.1.call-done.refs_0_.refs_1_.refs_2_.refs_3_, bf16[1024,4096]{1,0:T(8,128)(2,1)} %all-gather.7.cloned.1.call-done.refs_0_.refs_1_.refs_2_.refs_3_, ...), custom_call_target="tpu_custom_call" | custom-call | flops 42949672960 | bytes 60817408 | tf_op jit(solution)/shard_map/pallas_call | solution.py:57
  1117.1 56.6 %collective-permute-done.34.refs_0_ = bf16[1280,1024]{1,0:T(8,128)(2,1)S(1)} collective-permute-done((bf16[1280,1024]{1,0:T(8,128)(2,1)}, bf16[1280,1024]{1,0:T(8,128)(2,1)S(1)}, u32[]{:S(2)}, u32[]{:S(2)}) %collective-permute-start.34) | collective-permute-done | bytes 2621472 | tf_op jit(solution)/shard_map/ppermute | solution.py:343
  1176.0 53.9 %collective-permute-done.35.refs_1_ = bf16[1280,1024]{1,0:T(8,128)(2,1)S(1)} collective-permute-done((bf16[1280,1024]{1,0:T(8,128)(2,1)}, bf16[1280,1024]{1,0:T(8,128)(2,1)S(1)}, u32[]{:S(2)}, u32[]{:S(2)}) %collective-permute-start.35) | collective-permute-done | bytes 2621472 | tf_op jit(solution)/shard_map/ppermute | solution.py:343
  1253.8 55.9 %shard_map.86.q_ref.k_ref.v_ref = bf16[2,1024,2560]{2,1,0:T(8,128)(2,1)} custom-call(s32[4]{0:T(128)} %pad_add_fusion.ids_ref, bf16[1024,4096]{1,0:T(8,128)(2,1)} %all-gather.11.cloned.1.call-done.refs_0_.refs_1_.refs_2_.refs_3_, bf16[1024,4096]{1,0:T(8,128)(2,1)} %all-gather.11.cloned.1.call-done.refs_0_.refs_1_.refs_2_.refs_3_, ...), custom_call_target="tpu_custom_call" | custom-call | flops 42949672960 | bytes 60817408 | tf_op jit(solution)/shard_map/pallas_call | solution.py:57
  1325.6 17.5 %shard_map.88 = bf16[1024,2048]{1,0:T(8,128)(2,1)} custom-call(bf16[2,1024,256]{2,1,0:T(8,128)(2,1)} %shard_map.87.a_ref, bf16[2,1024,1024]{2,1,0:T(8,128)(2,1)} %fusion.16.m_ref, bf16[1280,1024]{1,0:T(8,128)(2,1)} %get-tuple-element.42.refs_0_, bf16[1280,1024]{1,0:T(8,128)(2,1)} %collective-permute-done.31.refs_1_, bf16[1280,1024]{1,0:T(8,128)(2,1)} %copy-done.16, ...), custom_call_target="tpu_custom_call" | custom-call | flops 10737418240 | bytes 19922944 | tf_op jit(solution)/shard_map/pallas_call | solution.py:91
  1343.2 17.7 %shard_map.89 = bf16[1024,2048]{1,0:T(8,128)(2,1)} custom-call(bf16[2,1024,256]{2,1,0:T(8,128)(2,1)} %shard_map.87.a_ref, bf16[2,1024,1024]{2,1,0:T(8,128)(2,1)} %fusion.16.m_ref, bf16[1280,1024]{1,0:T(8,128)(2,1)} %copy-done.19, bf16[1280,1024]{1,0:T(8,128)(2,1)} %copy-done.20, bf16[1280,1024]{1,0:T(8,128)(2,1)} %copy-done.22, ...), custom_call_target="tpu_custom_call" | custom-call | flops 10737418240 | bytes 19922944 | tf_op jit(solution)/shard_map/pallas_call | solution.py:91
  1393.5 42.1 %reduce-scatter.23.cloned.1.call-done.refs_11_ = bf16[256,2048]{1,0:T(8,128)(2,1)} async-done(((bf16[1024,2048]{1,0:T(8,128)(2,1)}), bf16[256,2048]{1,0:T(8,128)(2,1)}) %reduce-scatter.23.cloned.1.call-update) | async-done | bytes 1048592 | tf_op jit(solution)/shard_map/reduce_scatter | solution.py:415
  (219 shorter events, 396.4 us)
Async XLA Ops:
  6.5 285.3 %all-gather.5.cloned.1.call-start = ((), (), s32[]{:S(2)}) async-start(), calls=%async_computation.8 | async-start | bytes 10485760 | tf_op jit(solution)/shard_map/all_gather | solution.py:396
  48.8 485.2 %all-gather.9.cloned.1.call-start = ((), (), s32[]{:S(2)}) async-start(), calls=%async_computation.14 | async-start | bytes 10485760 | tf_op jit(solution)/shard_map/all_gather | solution.py:396
  57.7 114.0 %collective-permute-start.4 = (bf16[1024,2560]{1,0:T(8,128)(2,1)}, bf16[1024,2560]{1,0:T(8,128)(2,1)}, u32[]{:S(2)}, u32[]{:S(2)}) collective-permute-start(bf16[1024,2560]{1,0:T(8,128)(2,1)} %get-tuple-element.40), channel_id=1, source_target_pairs={{0,8},{1,9},{2,10},{3,11},{4,12},{5,13},{6,14},{7,15},{8,0},{9,1},... | collective-permute-start | bytes 15728648 | tf_op jit(solution)/shard_map/ppermute | solution.py:343
  58.9 148.3 %collective-permute-start.7 = (bf16[1024,2560]{1,0:T(8,128)(2,1)}, bf16[1024,2560]{1,0:T(8,128)(2,1)}, u32[]{:S(2)}, u32[]{:S(2)}) collective-permute-start(bf16[1024,2560]{1,0:T(8,128)(2,1)} %get-tuple-element.39.refs_3_), channel_id=1, source_target_pairs={{0,24},{1,25},{2,26},{3,27},{4,28},{5,29},{6,30},{7,31},{8,16},{9,... | collective-permute-start | bytes 15728648 | tf_op jit(solution)/shard_map/ppermute | solution.py:343
  171.7 114.6 %collective-permute-start.5 = (bf16[1024,2560]{1,0:T(8,128)(2,1)}, bf16[1024,2560]{1,0:T(8,128)(2,1)}, u32[]{:S(2)}, u32[]{:S(2)}) collective-permute-start(bf16[1024,2560]{1,0:T(8,128)(2,1)} %collective-permute-done.4.refs_4_), channel_id=1, source_target_pairs={{0,24},{1,25},{2,26},{3,27},{4,28},{5,29},{6,30},{7,31},{8,16},{9,... | collective-permute-start | bytes 15728648 | tf_op jit(solution)/shard_map/ppermute | solution.py:343
  206.3 456.7 %reduce-scatter.9.cloned.1.call-start = ((), (), s32[]{:S(2)}) async-start(), calls=%async_computation.9 | async-start | bytes 5242880 | tf_op jit(solution)/shard_map/reduce_scatter | solution.py:415
  392.9 270.2 %reduce-scatter.11.cloned.1.call-start = ((), (), s32[]{:S(2)}) async-start(), calls=%async_computation.10 | async-start | bytes 5242880 | tf_op jit(solution)/shard_map/reduce_scatter | solution.py:415
  395.7 113.3 %collective-permute-start.16 = (bf16[1280,1024]{1,0:T(8,128)(2,1)}, bf16[1280,1024]{1,0:T(8,128)(2,1)S(1)}, u32[]{:S(2)}, u32[]{:S(2)}) collective-permute-start(bf16[1280,1024]{1,0:T(8,128)(2,1)} %collective-permute-done.12.refs_1_), channel_id=1, source_target_pairs={{0,24},{1,25},{2,26},{3,27},{4,28},{5,29},{6,30},{7,31},{8,16},{9,... | collective-permute-start | bytes 7864328 | tf_op jit(solution)/shard_map/ppermute | solution.py:343
  532.2 313.6 %reduce-scatter.17.cloned.1.call-start = ((), (), s32[]{:S(2)}) async-start(), calls=%async_computation.15 | async-start | bytes 5242880 | tf_op jit(solution)/shard_map/reduce_scatter | solution.py:415
  633.6 212.4 %reduce-scatter.19.cloned.1.call-start = ((), (), s32[]{:S(2)}) async-start(), calls=%async_computation.16 | async-start | bytes 5242880 | tf_op jit(solution)/shard_map/reduce_scatter | solution.py:415
  651.3 371.9 %all-gather.7.cloned.1.call-start = ((), (), s32[]{:S(2)}) async-start(), calls=%async_computation.11 | async-start | bytes 10485760 | tf_op jit(solution)/shard_map/all_gather | solution.py:396
  718.9 534.9 %all-gather.11.cloned.1.call-start = ((), (), s32[]{:S(2)}) async-start(), calls=%async_computation.17 | async-start | bytes 10485760 | tf_op jit(solution)/shard_map/all_gather | solution.py:396
  728.0 115.2 %collective-permute-start.23 = (bf16[1024,2560]{1,0:T(8,128)(2,1)}, bf16[1024,2560]{1,0:T(8,128)(2,1)}, u32[]{:S(2)}, u32[]{:S(2)}) collective-permute-start(bf16[1024,2560]{1,0:T(8,128)(2,1)} %get-tuple-element.37), channel_id=1, source_target_pairs={{0,8},{1,9},{2,10},{3,11},{4,12},{5,13},{6,14},{7,15},{8,0},{9,1},... | collective-permute-start | bytes 15728648 | tf_op jit(solution)/shard_map/ppermute | solution.py:343
  728.0 174.0 %collective-permute-start.24 = (bf16[1024,2560]{1,0:T(8,128)(2,1)}, bf16[1024,2560]{1,0:T(8,128)(2,1)}, u32[]{:S(2)}, u32[]{:S(2)}) collective-permute-start(bf16[1024,2560]{1,0:T(8,128)(2,1)} %get-tuple-element.38.refs_4_), channel_id=1, source_target_pairs={{0,24},{1,25},{2,26},{3,27},{4,28},{5,29},{6,30},{7,31},{8,16},{9,... | collective-permute-start | bytes 15728648 | tf_op jit(solution)/shard_map/ppermute | solution.py:343
  843.2 115.5 %collective-permute-start.25 = (bf16[1024,2560]{1,0:T(8,128)(2,1)}, bf16[1024,2560]{1,0:T(8,128)(2,1)}, u32[]{:S(2)}, u32[]{:S(2)}) collective-permute-start(bf16[1024,2560]{1,0:T(8,128)(2,1)} %collective-permute-done.23.refs_5_), channel_id=1, source_target_pairs={{0,24},{1,25},{2,26},{3,27},{4,28},{5,29},{6,30},{7,31},{8,16},{9,... | collective-permute-start | bytes 15728648 | tf_op jit(solution)/shard_map/ppermute | solution.py:343
  854.4 105.8 %collective-permute-start.30 = (bf16[1280,1024]{1,0:T(8,128)(2,1)}, bf16[1280,1024]{1,0:T(8,128)(2,1)}, u32[]{:S(2)}, u32[]{:S(2)}) collective-permute-start(bf16[1280,1024]{1,0:T(8,128)(2,1)} %get-tuple-element.32), channel_id=1, source_target_pairs={{0,1},{1,0},{2,3},{3,2},{4,5},{5,4},{6,7},{7,6},{8,9},{9,8},{10,11... | collective-permute-start | bytes 7864328 | tf_op jit(solution)/shard_map/ppermute | solution.py:343
  901.1 462.8 %reduce-scatter.13.cloned.1.call-start = ((), (), s32[]{:S(2)}) async-start(), calls=%async_computation.12 | async-start | bytes 5242880 | tf_op jit(solution)/shard_map/reduce_scatter | solution.py:415
  901.2 122.0 %collective-permute-start.26 = (bf16[1024,2560]{1,0:T(8,128)(2,1)}, bf16[1024,2560]{1,0:T(8,128)(2,1)}, u32[]{:S(2)}, u32[]{:S(2)}) collective-permute-start(bf16[1024,2560]{1,0:T(8,128)(2,1)} %get-tuple-element.38.refs_4_), channel_id=1, source_target_pairs={{0,1},{1,0},{2,3},{3,2},{4,5},{5,4},{6,7},{7,6},{8,9},{9,8},{10,11... | collective-permute-start | bytes 15728648 | tf_op jit(solution)/shard_map/ppermute | solution.py:343
  901.9 121.3 %collective-permute-start.27 = (bf16[1024,2560]{1,0:T(8,128)(2,1)}, bf16[1024,2560]{1,0:T(8,128)(2,1)}, u32[]{:S(2)}, u32[]{:S(2)}) collective-permute-start(bf16[1024,2560]{1,0:T(8,128)(2,1)} %collective-permute-done.23.refs_5_), channel_id=1, source_target_pairs={{0,1},{1,0},{2,3},{3,2},{4,5},{5,4},{6,7},{7,6},{8,9},{9,8},{10,11... | collective-permute-start | bytes 15728648 | tf_op jit(solution)/shard_map/ppermute | solution.py:343
  902.0 121.2 %collective-permute-start.28 = (bf16[1024,2560]{1,0:T(8,128)(2,1)}, bf16[1024,2560]{1,0:T(8,128)(2,1)}, u32[]{:S(2)}, u32[]{:S(2)}) collective-permute-start(bf16[1024,2560]{1,0:T(8,128)(2,1)} %collective-permute-done.24.refs_6_), channel_id=1, source_target_pairs={{0,1},{1,0},{2,3},{3,2},{4,5},{5,4},{6,7},{7,6},{8,9},{9,8},{10,11... | collective-permute-start | bytes 15728648 | tf_op jit(solution)/shard_map/ppermute | solution.py:343
  1114.2 253.7 %reduce-scatter.15.cloned.1.call-start = ((), (), s32[]{:S(2)}) async-start(), calls=%async_computation.13 | async-start | bytes 5242880 | tf_op jit(solution)/shard_map/reduce_scatter | solution.py:415
  1117.0 112.9 %collective-permute-start.35 = (bf16[1280,1024]{1,0:T(8,128)(2,1)}, bf16[1280,1024]{1,0:T(8,128)(2,1)S(1)}, u32[]{:S(2)}, u32[]{:S(2)}) collective-permute-start(bf16[1280,1024]{1,0:T(8,128)(2,1)} %collective-permute-done.31.refs_1_), channel_id=1, source_target_pairs={{0,24},{1,25},{2,26},{3,27},{4,28},{5,29},{6,30},{7,31},{8,16},{9,... | collective-permute-start | bytes 7864328 | tf_op jit(solution)/shard_map/ppermute | solution.py:343
  1253.5 135.9 %reduce-scatter.21.cloned.1.call-start = ((), (), s32[]{:S(2)}) async-start(), calls=%async_computation.18 | async-start | bytes 5242880 | tf_op jit(solution)/shard_map/reduce_scatter | solution.py:415
  1343.2 92.4 %reduce-scatter.23.cloned.1.call-start = ((), (), s32[]{:S(2)}) async-start(), calls=%async_computation.19 | async-start | bytes 5242880 | tf_op jit(solution)/shard_map/reduce_scatter | solution.py:415
  (62 other events, 2496.1 us)
Sparse Core Ops, SparseCore 0:
  48.9 81.3 all-gather.4
  206.4 79.9 all-gather.8
  393.0 45.2 reduce-scatter.8
  532.4 45.4 reduce-scatter.10
  633.7 45.6 reduce-scatter.16
  681.6 44.0 reduce-scatter.18
  727.2 80.1 all-gather.6
  901.2 79.6 all-gather.10
  1114.3 45.7 reduce-scatter.12
  1253.6 45.6 reduce-scatter.14
  1343.3 46.0 reduce-scatter.20
  1391.5 43.9 reduce-scatter.22

commit v3 on v2

--- a/solution.py
+++ b/solution.py
@@ -18,7 +18,7 @@
     n_slabs = len(ours)
     rows, cols = h_seq.shape[0], ours[0].shape[1]
     depth = ours[0].shape[0]
-    tile, chunk = 512, 512
+    tile, chunk = 512, 1024
     tiles = cols // tile
     out_dtype = jnp.bfloat16 if final else jnp.float32
 
@@ -29,9 +29,9 @@
             @pl.loop(0, rows // chunk)
             def _(step):
                 at = pl.ds(pl.multiple_of(step * chunk, chunk), chunk)
-                total = matmul(h_refs[0][at, :], w_half[0][...])
-                for h_ref, w_ref in zip(h_refs[1:], w_half[1:]):
-                    total = total + matmul(h_ref[at, :], w_ref[...])
+                lhs = jnp.concatenate([h_ref[at, :] for h_ref in h_refs], axis=1)
+                rhs = jnp.concatenate([w_ref[...] for w_ref in w_half], axis=0)
+                total = matmul(lhs, rhs)
                 if len(rest) == 2:
                     total = total + rest[0][0, at, :]
                 rest[-1][0, at, :] = total.astype(out_dtype)
@@ -67,7 +67,7 @@
     ff = mlp.shape[2]
     n_slabs = len(ours)
     depth, cols = ours[0].shape
-    tile, chunk = 512, 512
+    tile, chunk = 512, 1024
     tiles = cols // tile
 
     def kernel(a_ref, m_ref, *refs):
@@ -80,9 +80,9 @@
                 @pl.loop(0, rows // chunk)
                 def _(step):
                     at = pl.ds(pl.multiple_of(step * chunk, chunk), chunk)
-                    total = matmul(m_ref[0, at, :], wa_ref[q_cut:, :]) + matmul(m_ref[1, at, :], wb_ref[q_cut:, :])
-                    total = total + matmul(a_ref[0, at, :], wa_ref[:q_cut, :]) + matmul(a_ref[1, at, :], wb_ref[:q_cut, :])
-                    out_ref[at, :] = total.astype(jnp.bfloat16)
+                    lhs = jnp.concatenate([a_ref[0, at, :], m_ref[0, at, :], a_ref[1, at, :], m_ref[1, at, :]], axis=1)
+                    rhs = jnp.concatenate([wa_ref[...], wb_ref[...]], axis=0)
+                    out_ref[at, :] = matmul(lhs, rhs).astype(jnp.bfloat16)
 
     def w_spec(i):
         return pl.BlockSpec((depth, tile), lambda s, n: (0, jnp.where(s == i, n, jnp.where(s < i, 0, tiles - 1))))
@@ -358,7 +358,12 @@
         slabs = (row, row ^ 1, last - row, (last - row) ^ 1)
 
         work_lens = jnp.where(even, len_loc, send(len_loc, near_swap))
-        gain_all = lax.all_gather(gain_loc, 'data', axis=1, tiled=True)
+        gain_near = send(gain_loc, near_swap)
+        gain_far = send(gain_loc, far_swap)
+        gain_fn = send(gain_near, far_swap)
+        gain_all = jnp.zeros((n_layers, n_data * slab), gain_loc.dtype)
+        for s, g in zip(slabs, (gain_loc, gain_near, gain_far, gain_fn)):
+            gain_all = lax.dynamic_update_slice_in_dim(gain_all, g, s * slab, axis=1)
 
         def pieces(keep_half, give_half):
             other = send(give_half, core_swap)

time: 1500 us -> 1480 us (0.987)
  blocking collectives: 16.6 us -> 0 us
    all_gather x1 -> x0, blocking collectives: 16.6 us -> none  [two_layers(): gain_all = lax.all_gather(gain_loc, 'data', axis=1, tiled=True)]
    ppermute x51 -> x54, waiting for transfers between devices: 762 us -> 773 us  [send(): return lax.ppermute(val, BOTH, pairs)]
    ppermute x51 -> x54, starting transfers between devices: 58.2 us -> 63.9 us  [send(): return lax.ppermute(val, BOTH, pairs)]
  transfers between devices with their start and end apart: 63 -> 66, of which waited for: 24 -> 26; matrix products, arithmetic and copies ran while one was open for 5% -> 5% of each run, Pallas kernels for 33% -> 32%
where the time goes in v3:
time: 1480 us; the launch traced here: 1470 us
  waiting for transfers between devices  827 us (56%)
  Pallas kernels  478 us (32%)
  other arithmetic  66.2 us (4%)
  starting transfers between devices  64.6 us (4%)
  local copies, waits for them, and re-layouts  21.6 us (1%)
    ppermute x54, waiting for transfers between devices, send(): return lax.ppermute(val, BOTH, pairs)  773 us
    pallas_call x6, Pallas kernels, project(): pl.pallas_call(kernel, out_shape=out_shape, grid_spec=pltpu.PrefetchScala...  235 us
    pallas_call x8, Pallas kernels, mix_out(): pl.pallas_call(kernel, out_shape=jax.ShapeDtypeStruct((rows, n_slabs * co...  136 us
    ppermute x54, starting transfers between devices, send(): return lax.ppermute(val, BOTH, pairs)  63.9 us
    reduce_scatter x8, waiting for transfers between devices, two_layers(): lax.psum_scatter(part, 'model', scatter_dimension=0, tiled=True, axis_ind...  53.9 us
    pallas_call x4, Pallas kernels, attend(): pl.pallas_call(kernel, out_shape=jax.ShapeDtypeStruct((2, rows, head_dim)...  38.9 us
  transfers between devices with their start and end apart: 66, of which 26 were waited for; matrix products, arithmetic and copies ran while one was open for 5% of the time, Pallas kernels for 32%

profile of v3, /device:TPU:97, one launch (start us, length us, event | category | flops | bytes accessed | tf_op | source)
XLA Modules:
  0.0 1472.4 jit_solution(10884187278668100929)
XLA Ops:
  59.1 112.6 %collective-permute-done.7.refs_4_ = bf16[1024,2560]{1,0:T(8,128)(2,1)} collective-permute-done((bf16[1024,2560]{1,0:T(8,128)(2,1)}, bf16[1024,2560]{1,0:T(8,128)(2,1)}, u32[]{:S(2)}, u32[]{:S(2)}) %collective-permute-start.7) | collective-permute-done | bytes 5242912 | tf_op jit(solution)/shard_map/ppermute | solution.py:343
  212.7 74.8 %collective-permute-done.8.refs_1_ = bf16[1024,2560]{1,0:T(8,128)(2,1)} collective-permute-done((bf16[1024,2560]{1,0:T(8,128)(2,1)}, bf16[1024,2560]{1,0:T(8,128)(2,1)}, u32[]{:S(2)}, u32[]{:S(2)}) %collective-permute-start.8) | collective-permute-done | bytes 5242912 | tf_op jit(solution)/shard_map/ppermute | solution.py:343
  291.6 42.2 %shard_map.66.refs_3_ = f32[2,1024,2560]{2,1,0:T(8,128)} custom-call(s32[3]{0:T(128)} %pad_add_fusion.2.ids_ref, bf16[1024,4096]{1,0:T(8,128)(2,1)} %all-gather.5.cloned.1.call-done.refs_0_.refs_1_.refs_2_, bf16[1024,4096]{1,0:T(8,128)(2,1)} %all-gather.5.cloned.1.call-done.refs_0_.refs_1_.refs_2_, ...), custom_call_target="tpu_custom_call" | custom-call | flops 32212254720 | bytes 48234496 | tf_op jit(solution)/shard_map/pallas_call | solution.py:57
  333.8 21.3 %shard_map.67.q_ref.k_ref.v_ref = bf16[2,1024,2560]{2,1,0:T(8,128)(2,1)} custom-call(s32[1]{0:T(128)} %bitcast.3.ids_ref, bf16[1024,4096]{1,0:T(8,128)(2,1)} %all-gather.5.cloned.1.call-done.refs_0_.refs_1_.refs_2_, bf16[1024,2560]{1,0:T(8,128)(2,1)} %collective-permute-done.8.refs_1_, bf16[1024,2560]{1,0:T(8,128)(2,1)} %collective-permute-done.9.refs_2_, ...), custom_call_target="tpu_custom_call" | custom-call | flops 10737418240 | bytes 23068672 | tf_op jit(solution)/shard_map/pallas_call | solution.py:57
  392.4 57.1 %collective-permute-done.18.refs_0_ = bf16[1280,1024]{1,0:T(8,128)(2,1)S(1)} collective-permute-done((bf16[1280,1024]{1,0:T(8,128)(2,1)}, bf16[1280,1024]{1,0:T(8,128)(2,1)S(1)}, u32[]{:S(2)}, u32[]{:S(2)}) %collective-permute-start.18) | collective-permute-done | bytes 2621472 | tf_op jit(solution)/shard_map/ppermute | solution.py:343
  451.0 54.6 %collective-permute-done.19.refs_1_ = bf16[1280,1024]{1,0:T(8,128)(2,1)S(1)} collective-permute-done((bf16[1280,1024]{1,0:T(8,128)(2,1)}, bf16[1280,1024]{1,0:T(8,128)(2,1)S(1)}, u32[]{:S(2)}, u32[]{:S(2)}) %collective-permute-start.19) | collective-permute-done | bytes 2621472 | tf_op jit(solution)/shard_map/ppermute | solution.py:343
  511.3 17.0 %shard_map.71 = bf16[1024,2048]{1,0:T(8,128)(2,1)} custom-call(bf16[2,1024,256]{2,1,0:T(8,128)(2,1)} %shard_map.68.a_ref, bf16[2,1024,1024]{2,1,0:T(8,128)(2,1)} %fusion.19.m_ref, bf16[1280,1024]{1,0:T(8,128)(2,1)} %copy-done.17, bf16[1280,1024]{1,0:T(8,128)(2,1)} %copy-done.18, bf16[1280,1024]{1,0:T(8,128)(2,1)} %copy-done.21, ...), custom_call_target="tpu_custom_call" | custom-call | flops 10737418240 | bytes 19922944 | tf_op jit(solution)/shard_map/pallas_call | solution.py:91
  529.6 42.0 %shard_map.80.refs_3_ = f32[2,1024,2560]{2,1,0:T(8,128)} custom-call(s32[3]{0:T(128)} %pad_add_fusion.2.ids_ref, bf16[1024,4096]{1,0:T(8,128)(2,1)} %all-gather.9.cloned.1.call-done.refs_0_.refs_1_.refs_2_, bf16[1024,4096]{1,0:T(8,128)(2,1)} %all-gather.9.cloned.1.call-done.refs_0_.refs_1_.refs_2_, ...), custom_call_target="tpu_custom_call" | custom-call | flops 32212254720 | bytes 48234496 | tf_op jit(solution)/shard_map/pallas_call | solution.py:57
  571.6 21.3 %shard_map.81.q_ref.k_ref.v_ref = bf16[2,1024,2560]{2,1,0:T(8,128)(2,1)} custom-call(s32[1]{0:T(128)} %bitcast.3.ids_ref, bf16[1024,4096]{1,0:T(8,128)(2,1)} %all-gather.9.cloned.1.call-done.refs_0_.refs_1_.refs_2_, bf16[1024,2560]{1,0:T(8,128)(2,1)} %collective-permute-done.8.refs_1_, bf16[1024,2560]{1,0:T(8,128)(2,1)} %collective-permute-done.9.refs_2_, ...), custom_call_target="tpu_custom_call" | custom-call | flops 10737418240 | bytes 23068672 | tf_op jit(solution)/shard_map/pallas_call | solution.py:57
  608.8 16.9 %shard_map.83 = bf16[1024,2048]{1,0:T(8,128)(2,1)} custom-call(bf16[2,1024,256]{2,1,0:T(8,128)(2,1)} %shard_map.82.a_ref, bf16[2,1024,1024]{2,1,0:T(8,128)(2,1)} %fusion.17.m_ref, bf16[1280,1024]{1,0:T(8,128)(2,1)} %get-tuple-element.44.refs_0_, bf16[1280,1024]{1,0:T(8,128)(2,1)} %collective-permute-done.15.refs_1_, bf16[1280,1024]{1,0:T(8,128)(2,1)} %copy-done.15, ...), custom_call_target="tpu_custom_call" | custom-call | flops 10737418240 | bytes 19922944 | tf_op jit(solution)/shard_map/pallas_call | solution.py:91
  625.8 17.3 %shard_map.84 = bf16[1024,2048]{1,0:T(8,128)(2,1)} custom-call(bf16[2,1024,256]{2,1,0:T(8,128)(2,1)} %shard_map.82.a_ref, bf16[2,1024,1024]{2,1,0:T(8,128)(2,1)} %fusion.17.m_ref, bf16[1280,1024]{1,0:T(8,128)(2,1)} %copy-done.17, bf16[1280,1024]{1,0:T(8,128)(2,1)} %copy-done.18, bf16[1280,1024]{1,0:T(8,128)(2,1)} %copy-done.21, ...), custom_call_target="tpu_custom_call" | custom-call | flops 10737418240 | bytes 19922944 | tf_op jit(solution)/shard_map/pallas_call | solution.py:91
  657.1 23.7 %collective-permute-done.22.refs_2_ = bf16[256,2048]{1,0:T(8,128)(2,1)S(1)} collective-permute-done((bf16[256,2048]{1,0:T(8,128)(2,1)}, bf16[256,2048]{1,0:T(8,128)(2,1)S(1)}, u32[]{:S(2)}, u32[]{:S(2)}) %collective-permute-start.22) | collective-permute-done | bytes 1048608 | tf_op jit(solution)/shard_map/ppermute | solution.py:343
  680.8 22.0 %collective-permute-done.23.refs_3_ = bf16[256,2048]{1,0:T(8,128)(2,1)S(1)} collective-permute-done((bf16[256,2048]{1,0:T(8,128)(2,1)}, bf16[256,2048]{1,0:T(8,128)(2,1)S(1)}, u32[]{:S(2)}, u32[]{:S(2)}) %collective-permute-start.23) | collective-permute-done | bytes 1048608 | tf_op jit(solution)/shard_map/ppermute | solution.py:343
  722.1 112.6 %collective-permute-done.26.refs_5_ = bf16[1024,2560]{1,0:T(8,128)(2,1)} collective-permute-done((bf16[1024,2560]{1,0:T(8,128)(2,1)}, bf16[1024,2560]{1,0:T(8,128)(2,1)}, u32[]{:S(2)}, u32[]{:S(2)}) %collective-permute-start.26) | collective-permute-done | bytes 5242912 | tf_op jit(solution)/shard_map/ppermute | solution.py:343
  863.0 22.5 %collective-permute-done.48.refs_3_ = bf16[256,2048]{1,0:T(8,128)(2,1)} collective-permute-done((bf16[256,2048]{1,0:T(8,128)(2,1)}, bf16[256,2048]{1,0:T(8,128)(2,1)}, u32[]{:S(2)}, u32[]{:S(2)}) %collective-permute-start.48) | collective-permute-done | bytes 1048608 | tf_op jit(solution)/shard_map/ppermute | solution.py:343
  893.8 56.4 %collective-permute-done.28.refs_7_ = bf16[1024,2560]{1,0:T(8,128)(2,1)} collective-permute-done((bf16[1024,2560]{1,0:T(8,128)(2,1)}, bf16[1024,2560]{1,0:T(8,128)(2,1)}, u32[]{:S(2)}, u32[]{:S(2)}) %collective-permute-start.28) | collective-permute-done | bytes 5242912 | tf_op jit(solution)/shard_map/ppermute | solution.py:343
  955.3 58.5 %collective-permute-done.34.refs_1_ = bf16[1280,1024]{1,0:T(8,128)(2,1)} collective-permute-done((bf16[1280,1024]{1,0:T(8,128)(2,1)S(1)}, bf16[1280,1024]{1,0:T(8,128)(2,1)}, u32[]{:S(2)}, u32[]{:S(2)}) %collective-permute-start.34) | collective-permute-done | bytes 2621472 | tf_op jit(solution)/shard_map/ppermute | solution.py:343
  1014.8 54.3 %shard_map.74.q_ref.k_ref.v_ref = bf16[2,1024,2560]{2,1,0:T(8,128)(2,1)} custom-call(s32[4]{0:T(128)} %pad_add_fusion.ids_ref, bf16[1024,4096]{1,0:T(8,128)(2,1)} %all-gather.7.cloned.1.call-done.refs_0_.refs_1_.refs_2_.refs_3_, bf16[1024,4096]{1,0:T(8,128)(2,1)} %all-gather.7.cloned.1.call-done.refs_0_.refs_1_.refs_2_.refs_3_, ...), custom_call_target="tpu_custom_call" | custom-call | flops 42949672960 | bytes 60817408 | tf_op jit(solution)/shard_map/pallas_call | solution.py:57
  1106.1 56.7 %collective-permute-done.37.refs_0_ = bf16[1280,1024]{1,0:T(8,128)(2,1)S(1)} collective-permute-done((bf16[1280,1024]{1,0:T(8,128)(2,1)}, bf16[1280,1024]{1,0:T(8,128)(2,1)S(1)}, u32[]{:S(2)}, u32[]{:S(2)}) %collective-permute-start.37) | collective-permute-done | bytes 2621472 | tf_op jit(solution)/shard_map/ppermute | solution.py:343
  1165.1 53.9 %collective-permute-done.38.refs_1_ = bf16[1280,1024]{1,0:T(8,128)(2,1)S(1)} collective-permute-done((bf16[1280,1024]{1,0:T(8,128)(2,1)}, bf16[1280,1024]{1,0:T(8,128)(2,1)S(1)}, u32[]{:S(2)}, u32[]{:S(2)}) %collective-permute-start.38) | collective-permute-done | bytes 2621472 | tf_op jit(solution)/shard_map/ppermute | solution.py:343
  1225.0 17.0 %shard_map.78 = bf16[1024,2048]{1,0:T(8,128)(2,1)} custom-call(bf16[2,1024,256]{2,1,0:T(8,128)(2,1)} %shard_map.75.a_ref, bf16[2,1024,1024]{2,1,0:T(8,128)(2,1)} %fusion.18.m_ref, bf16[1280,1024]{1,0:T(8,128)(2,1)} %copy-done.19, bf16[1280,1024]{1,0:T(8,128)(2,1)} %copy-done.20, bf16[1280,1024]{1,0:T(8,128)(2,1)} %copy-done.22, ...), custom_call_target="tpu_custom_call" | custom-call | flops 10737418240 | bytes 19922944 | tf_op jit(solution)/shard_map/pallas_call | solution.py:91
  1242.2 54.1 %shard_map.86.q_ref.k_ref.v_ref = bf16[2,1024,2560]{2,1,0:T(8,128)(2,1)} custom-call(s32[4]{0:T(128)} %pad_add_fusion.ids_ref, bf16[1024,4096]{1,0:T(8,128)(2,1)} %all-gather.11.cloned.1.call-done.refs_0_.refs_1_.refs_2_.refs_3_, bf16[1024,4096]{1,0:T(8,128)(2,1)} %all-gather.11.cloned.1.call-done.refs_0_.refs_1_.refs_2_.refs_3_, ...), custom_call_target="tpu_custom_call" | custom-call | flops 42949672960 | bytes 60817408 | tf_op jit(solution)/shard_map/pallas_call | solution.py:57
  1329.2 17.3 %shard_map.89 = bf16[1024,2048]{1,0:T(8,128)(2,1)} custom-call(bf16[2,1024,256]{2,1,0:T(8,128)(2,1)} %shard_map.87.a_ref, bf16[2,1024,1024]{2,1,0:T(8,128)(2,1)} %fusion.16.m_ref, bf16[1280,1024]{1,0:T(8,128)(2,1)} %copy-done.19, bf16[1280,1024]{1,0:T(8,128)(2,1)} %copy-done.20, bf16[1280,1024]{1,0:T(8,128)(2,1)} %copy-done.22, ...), custom_call_target="tpu_custom_call" | custom-call | flops 10737418240 | bytes 19922944 | tf_op jit(solution)/shard_map/pallas_call | solution.py:91
  1378.9 42.1 %reduce-scatter.23.cloned.1.call-done.refs_11_ = bf16[256,2048]{1,0:T(8,128)(2,1)} async-done(((bf16[1024,2048]{1,0:T(8,128)(2,1)}), bf16[256,2048]{1,0:T(8,128)(2,1)}) %reduce-scatter.23.cloned.1.call-update) | async-done | bytes 1048592 | tf_op jit(solution)/shard_map/reduce_scatter | solution.py:420
  (229 shorter events, 389.9 us)
Async XLA Ops:
  6.5 285.1 %all-gather.5.cloned.1.call-start = ((), (), s32[]{:S(2)}) async-start(), calls=%async_computation.8 | async-start | bytes 10485760 | tf_op jit(solution)/shard_map/all_gather | solution.py:401
  47.5 482.1 %all-gather.9.cloned.1.call-start = ((), (), s32[]{:S(2)}) async-start(), calls=%async_computation.14 | async-start | bytes 10485760 | tf_op jit(solution)/shard_map/all_gather | solution.py:401
  56.4 115.3 %collective-permute-start.7 = (bf16[1024,2560]{1,0:T(8,128)(2,1)}, bf16[1024,2560]{1,0:T(8,128)(2,1)}, u32[]{:S(2)}, u32[]{:S(2)}) collective-permute-start(bf16[1024,2560]{1,0:T(8,128)(2,1)} %get-tuple-element.40), channel_id=1, source_target_pairs={{0,8},{1,9},{2,10},{3,11},{4,12},{5,13},{6,14},{7,15},{8,0},{9,1},... | collective-permute-start | bytes 15728648 | tf_op jit(solution)/shard_map/ppermute | solution.py:343
  56.4 150.3 %collective-permute-start.10 = (bf16[1024,2560]{1,0:T(8,128)(2,1)}, bf16[1024,2560]{1,0:T(8,128)(2,1)}, u32[]{:S(2)}, u32[]{:S(2)}) collective-permute-start(bf16[1024,2560]{1,0:T(8,128)(2,1)} %get-tuple-element.39.refs_3_), channel_id=1, source_target_pairs={{0,24},{1,25},{2,26},{3,27},{4,28},{5,29},{6,30},{7,31},{8,16},{9,... | collective-permute-start | bytes 15728648 | tf_op jit(solution)/shard_map/ppermute | solution.py:343
  171.7 115.8 %collective-permute-start.8 = (bf16[1024,2560]{1,0:T(8,128)(2,1)}, bf16[1024,2560]{1,0:T(8,128)(2,1)}, u32[]{:S(2)}, u32[]{:S(2)}) collective-permute-start(bf16[1024,2560]{1,0:T(8,128)(2,1)} %collective-permute-done.7.refs_4_), channel_id=1, source_target_pairs={{0,24},{1,25},{2,26},{3,27},{4,28},{5,29},{6,30},{7,31},{8,16},{9,... | collective-permute-start | bytes 15728648 | tf_op jit(solution)/shard_map/ppermute | solution.py:343
  206.0 448.8 %reduce-scatter.9.cloned.1.call-start = ((), (), s32[]{:S(2)}) async-start(), calls=%async_computation.9 | async-start | bytes 5242880 | tf_op jit(solution)/shard_map/reduce_scatter | solution.py:420
  389.5 265.3 %reduce-scatter.11.cloned.1.call-start = ((), (), s32[]{:S(2)}) async-start(), calls=%async_computation.10 | async-start | bytes 5242880 | tf_op jit(solution)/shard_map/reduce_scatter | solution.py:420
  392.2 113.4 %collective-permute-start.19 = (bf16[1280,1024]{1,0:T(8,128)(2,1)}, bf16[1280,1024]{1,0:T(8,128)(2,1)S(1)}, u32[]{:S(2)}, u32[]{:S(2)}) collective-permute-start(bf16[1280,1024]{1,0:T(8,128)(2,1)} %collective-permute-done.15.refs_1_), channel_id=1, source_target_pairs={{0,24},{1,25},{2,26},{3,27},{4,28},{5,29},{6,30},{7,31},{8,16},{9,... | collective-permute-start | bytes 7864328 | tf_op jit(solution)/shard_map/ppermute | solution.py:343
  528.3 308.9 %reduce-scatter.17.cloned.1.call-start = ((), (), s32[]{:S(2)}) async-start(), calls=%async_computation.15 | async-start | bytes 5242880 | tf_op jit(solution)/shard_map/reduce_scatter | solution.py:420
  625.8 211.7 %reduce-scatter.19.cloned.1.call-start = ((), (), s32[]{:S(2)}) async-start(), calls=%async_computation.16 | async-start | bytes 5242880 | tf_op jit(solution)/shard_map/reduce_scatter | solution.py:420
  643.2 371.6 %all-gather.7.cloned.1.call-start = ((), (), s32[]{:S(2)}) async-start(), calls=%async_computation.11 | async-start | bytes 10485760 | tf_op jit(solution)/shard_map/all_gather | solution.py:401
  710.6 531.6 %all-gather.11.cloned.1.call-start = ((), (), s32[]{:S(2)}) async-start(), calls=%async_computation.17 | async-start | bytes 10485760 | tf_op jit(solution)/shard_map/all_gather | solution.py:401
  719.6 115.1 %collective-permute-start.26 = (bf16[1024,2560]{1,0:T(8,128)(2,1)}, bf16[1024,2560]{1,0:T(8,128)(2,1)}, u32[]{:S(2)}, u32[]{:S(2)}) collective-permute-start(bf16[1024,2560]{1,0:T(8,128)(2,1)} %get-tuple-element.37), channel_id=1, source_target_pairs={{0,8},{1,9},{2,10},{3,11},{4,12},{5,13},{6,14},{7,15},{8,0},{9,1},... | collective-permute-start | bytes 15728648 | tf_op jit(solution)/shard_map/ppermute | solution.py:343
  719.6 173.8 %collective-permute-start.27 = (bf16[1024,2560]{1,0:T(8,128)(2,1)}, bf16[1024,2560]{1,0:T(8,128)(2,1)}, u32[]{:S(2)}, u32[]{:S(2)}) collective-permute-start(bf16[1024,2560]{1,0:T(8,128)(2,1)} %get-tuple-element.38.refs_4_), channel_id=1, source_target_pairs={{0,24},{1,25},{2,26},{3,27},{4,28},{5,29},{6,30},{7,31},{8,16},{9,... | collective-permute-start | bytes 15728648 | tf_op jit(solution)/shard_map/ppermute | solution.py:343
  834.7 115.5 %collective-permute-start.28 = (bf16[1024,2560]{1,0:T(8,128)(2,1)}, bf16[1024,2560]{1,0:T(8,128)(2,1)}, u32[]{:S(2)}, u32[]{:S(2)}) collective-permute-start(bf16[1024,2560]{1,0:T(8,128)(2,1)} %collective-permute-done.26.refs_5_), channel_id=1, source_target_pairs={{0,24},{1,25},{2,26},{3,27},{4,28},{5,29},{6,30},{7,31},{8,16},{9,... | collective-permute-start | bytes 15728648 | tf_op jit(solution)/shard_map/ppermute | solution.py:343
  845.7 106.0 %collective-permute-start.33 = (bf16[1280,1024]{1,0:T(8,128)(2,1)}, bf16[1280,1024]{1,0:T(8,128)(2,1)}, u32[]{:S(2)}, u32[]{:S(2)}) collective-permute-start(bf16[1280,1024]{1,0:T(8,128)(2,1)} %get-tuple-element.32), channel_id=1, source_target_pairs={{0,1},{1,0},{2,3},{3,2},{4,5},{5,4},{6,7},{7,6},{8,9},{9,8},{10,11... | collective-permute-start | bytes 7864328 | tf_op jit(solution)/shard_map/ppermute | solution.py:343
  892.5 457.0 %reduce-scatter.13.cloned.1.call-start = ((), (), s32[]{:S(2)}) async-start(), calls=%async_computation.12 | async-start | bytes 5242880 | tf_op jit(solution)/shard_map/reduce_scatter | solution.py:420
  892.5 122.2 %collective-permute-start.29 = (bf16[1024,2560]{1,0:T(8,128)(2,1)}, bf16[1024,2560]{1,0:T(8,128)(2,1)}, u32[]{:S(2)}, u32[]{:S(2)}) collective-permute-start(bf16[1024,2560]{1,0:T(8,128)(2,1)} %get-tuple-element.38.refs_4_), channel_id=1, source_target_pairs={{0,1},{1,0},{2,3},{3,2},{4,5},{5,4},{6,7},{7,6},{8,9},{9,8},{10,11... | collective-permute-start | bytes 15728648 | tf_op jit(solution)/shard_map/ppermute | solution.py:343
  893.3 121.4 %collective-permute-start.30 = (bf16[1024,2560]{1,0:T(8,128)(2,1)}, bf16[1024,2560]{1,0:T(8,128)(2,1)}, u32[]{:S(2)}, u32[]{:S(2)}) collective-permute-start(bf16[1024,2560]{1,0:T(8,128)(2,1)} %collective-permute-done.26.refs_5_), channel_id=1, source_target_pairs={{0,1},{1,0},{2,3},{3,2},{4,5},{5,4},{6,7},{7,6},{8,9},{9,8},{10,11... | collective-permute-start | bytes 15728648 | tf_op jit(solution)/shard_map/ppermute | solution.py:343
  893.4 121.3 %collective-permute-start.31 = (bf16[1024,2560]{1,0:T(8,128)(2,1)}, bf16[1024,2560]{1,0:T(8,128)(2,1)}, u32[]{:S(2)}, u32[]{:S(2)}) collective-permute-start(bf16[1024,2560]{1,0:T(8,128)(2,1)} %collective-permute-done.27.refs_6_), channel_id=1, source_target_pairs={{0,1},{1,0},{2,3},{3,2},{4,5},{5,4},{6,7},{7,6},{8,9},{9,8},{10,11... | collective-permute-start | bytes 15728648 | tf_op jit(solution)/shard_map/ppermute | solution.py:343
  1103.3 250.2 %reduce-scatter.15.cloned.1.call-start = ((), (), s32[]{:S(2)}) async-start(), calls=%async_computation.13 | async-start | bytes 5242880 | tf_op jit(solution)/shard_map/reduce_scatter | solution.py:420
  1106.0 113.0 %collective-permute-start.38 = (bf16[1280,1024]{1,0:T(8,128)(2,1)}, bf16[1280,1024]{1,0:T(8,128)(2,1)S(1)}, u32[]{:S(2)}, u32[]{:S(2)}) collective-permute-start(bf16[1280,1024]{1,0:T(8,128)(2,1)} %collective-permute-done.34.refs_1_), channel_id=1, source_target_pairs={{0,24},{1,25},{2,26},{3,27},{4,28},{5,29},{6,30},{7,31},{8,16},{9,... | collective-permute-start | bytes 7864328 | tf_op jit(solution)/shard_map/ppermute | solution.py:343
  1242.1 132.8 %reduce-scatter.21.cloned.1.call-start = ((), (), s32[]{:S(2)}) async-start(), calls=%async_computation.18 | async-start | bytes 5242880 | tf_op jit(solution)/shard_map/reduce_scatter | solution.py:420
  1329.1 92.0 %reduce-scatter.23.cloned.1.call-start = ((), (), s32[]{:S(2)}) async-start(), calls=%async_computation.19 | async-start | bytes 5242880 | tf_op jit(solution)/shard_map/reduce_scatter | solution.py:420
  (65 other events, 2533.6 us)
Sparse Core Ops, SparseCore 0:
  47.6 81.2 all-gather.4
  206.1 79.2 all-gather.8
  389.6 45.2 reduce-scatter.8
  528.4 45.5 reduce-scatter.10
  625.9 45.5 reduce-scatter.16
  673.6 43.9 reduce-scatter.18
  719.2 80.1 all-gather.6
  892.6 79.6 all-gather.10
  1103.4 45.5 reduce-scatter.12
  1242.2 45.4 reduce-scatter.14
  1329.2 45.6 reduce-scatter.20
  1377.0 44.0 reduce-scatter.22
